TPU v7x, 32 devices: a whole 2x2x4 slice. The times are simulated.
32 devices in a mesh: gx: 2 (over x), gy: 4 (over y, core), gz: 4 (over z).
Axes of the slice: x: 2, y: 2, z: 4, core: 2. Of those that a mesh axis runs over, the one named last changes fastest.
Arguments:
- positions: float32 [3, 32768], P(None, ('gx', 'gy', 'gz')), may hold values from 0 to 16, as said below
- velocities: float32 [3, 32768], P(None, ('gx', 'gy', 'gz')), may hold values from -6 to 6
- inv_mass: float32 [32768], P(('gx', 'gy', 'gz')), may hold values from 0.5 to 2
- charge: float32 [32768], P(('gx', 'gy', 'gz')), may hold values from -4 to 4
- fast_force: float32 [3, 32768], P(None, ('gx', 'gy', 'gz')), may hold values from -6 to 6
- slow_force: float32 [3, 32768], P(None, ('gx', 'gy', 'gz')), may hold values from -6 to 6
- bonds: int32 [2, 32768], P(None, ('gx', 'gy', 'gz')), may hold values from 0 to 1023
- bond_k: float32 [32768], P(('gx', 'gy', 'gz')), may hold values from 0.05 to 0.4
- halo_index: int32 [6, 8192], P(None, ('gx', 'gy', 'gz')), may hold values from 0 to 1023
- pair_own: int32 [3072], P(('gx', 'gy', 'gz')), may hold values from 0 to 7
- pair_partner: int32 [3072], P(('gx', 'gy', 'gz')), may hold values from 0 to 19
- pair_count: int32 [32], P(('gx', 'gy', 'gz')), may hold values from 1 to 96
Outputs:
- displacement: float32 [3, 32768], P(None, ('gx', 'gy', 'gz'))
- velocities_out: float32 [3, 32768], P(None, ('gx', 'gy', 'gz'))
- fast_out: float32 [3, 32768], P(None, ('gx', 'gy', 'gz'))
- slow_out: float32 [3, 32768], P(None, ('gx', 'gy', 'gz'))
Inputs may be any that keep to these rules, and one draw needn't show every extreme that they name: `positions`: atoms of patch p lie in the cube of side 4 at 4 times its grid place.
All inputs are finite; a program needn't handle non-finite values.
Results may differ from a plain program's by a relative error of at most 0.0003.
Values sent between devices are 32-bit elements; how exact they have to be, the bound alone decides.
No kernel may reach another device: no remote copies, remote signals or barrier semaphores. Data moves between devices by JAX's collectives and lax.ppermute only.
A program may use at most 64 MiB of HBM per device.

v0:
```python
import functools

import jax
import jax.numpy as jnp
from jax import lax
from jax.experimental import pallas as pl
from jax.experimental.pallas import tpu as pltpu
from jax.sharding import PartitionSpec as P

AXES = ("gx", "gy", "gz")
INNER = 4
STEP = 0.1
SHORT_REACH = 0.64
LONG_REACH = 1.44
LONG_SCALE = 0.5
SIDE = 4.0
INV_LEN = 1.25
LEN = 0.8
LANES = 128
BLOCK = 256
FAR = -1.0e6
MAGIC = 32768.0

F32 = jnp.float32
BF16 = jnp.bfloat16


def matchings(sizes):
    nx, ny, nz = sizes
    assert nx % 2 == 0 and ny % 2 == 0 and nz % 2 == 0
    swaps = []
    for axis in (2, 0, 1):
        for phase in range(1 if sizes[axis] == 2 else 2):
            perm = []
            for a in range(nx):
                for b in range(ny):
                    for c in range(nz):
                        place = [a, b, c]
                        p = place[axis]
                        partner = p ^ 1 if phase == 0 else (p + 1 if p % 2 else p - 1)
                        if 0 <= partner < sizes[axis]:
                            place[axis] = partner
                        else:
                            other = 0 if axis == 1 else 1
                            place[other] ^= 1
                        perm.append(
                            ((a * ny + b) * nz + c, (place[0] * ny + place[1]) * nz + place[2])
                        )
            swaps.append((axis, phase, perm))
    return swaps


def rounded(a):
    return a.astype(BF16).astype(F32)


def split3(a):
    high = rounded(a)
    rest = a - high
    mid = rounded(rest)
    return high, mid, rounded(rest - mid)


def row_ids(shape):
    return lax.broadcasted_iota(jnp.int32, shape, 0)


def pick_rows(rows, shape):
    ids = row_ids(shape)
    out = jnp.zeros(shape, F32)
    for s, r in enumerate(rows):
        out = jnp.where(ids == s, r, out)
    return out


def centre(shape):
    parts = [lax.axis_index(ax).astype(F32) * SIDE + 0.5 * SIDE for ax in AXES]
    return pick_rows(parts, shape)


def scaled(x, mid):
    n = x.shape[1]
    full = jnp.concatenate([x[:3], jnp.zeros((5, n), F32)], axis=0)
    return (full - mid) * INV_LEN


def receiver_matrix(u):
    h, m, l = split3(u)
    norm = 1.0 - jnp.sum(u * u, axis=0, keepdims=True)
    a, b, c = split3(norm)
    h, m, l = 2.0 * h, 2.0 * m, 2.0 * l
    one = jnp.ones_like(norm)
    tail = pick_rows([a, b, c, one, one, one], u.shape)
    return jnp.concatenate([h, h, h, m, m, l, tail, jnp.zeros_like(u)], axis=0).astype(BF16)


def source_matrices(u, valid=None):
    h, m, l = split3(u)
    norm = -jnp.sum(u * u, axis=0, keepdims=True)
    if valid is not None:
        norm = jnp.where(valid, norm, FAR)
    a, b, c = split3(norm)
    one = jnp.ones_like(norm)
    tail = pick_rows([one, one, one, a, b, c], u.shape)
    pair = jnp.concatenate([h, m, l, h, m, h, tail, jnp.zeros_like(u)], axis=0)
    ids = row_ids(u.shape)
    total = jnp.concatenate([jnp.where(ids == 3, 1.0, h), m, l], axis=0).astype(BF16)
    return pair, total


def dot(a, b):
    return jnp.dot(a, b, preferred_element_type=F32)


def two_parts(w):
    high = (w + MAGIC) - MAGIC
    return high.astype(BF16), (w - high).astype(BF16)


def gather_lanes(sources, index):
    index = jnp.broadcast_to(index, (8, LANES))
    tile = lax.shift_right_logical(index, 7)
    lane = lax.bitwise_and(index, LANES - 1)
    out = jnp.zeros((8, LANES), F32)
    for r, src in enumerate(sources):
        out = jnp.where(tile == r, jnp.take_along_axis(src, lane, axis=1), out)
    return out


def lane_tiles(a):
    return [a[:, r * LANES : (r + 1) * LANES] for r in range(a.shape[1] // LANES)]


def pad8(x):
    return jnp.concatenate([x, jnp.zeros((8 - x.shape[0], x.shape[1]), F32)], axis=0)


def write_faces(swaps, x, charge, index_ref, send_refs):
    rows = [x] if charge is None else [x, charge]
    tiles = lane_tiles(pad8(jnp.concatenate(rows, axis=0)))
    for (axis, phase, _), ref in zip(swaps, send_refs):
        even = lax.axis_index(AXES[axis]) % 2 == 0
        high = even if phase == 0 else jnp.logical_not(even)
        index = jnp.where(high, index_ref[2 * axis + 1 : 2 * axis + 2, :], index_ref[2 * axis : 2 * axis + 1, :])
        for w in range(index.shape[1] // LANES):
            part = slice(w * LANES, (w + 1) * LANES)
            ref[:, part] = gather_lanes(tiles, index[:, part])[:4]


def start_kernel(swaps, x_ref, v_ref, mass_ref, fast_ref, slow_ref, index_ref, x_out, v_out, *send_refs):
    mass = mass_ref[...]
    v = v_ref[...] + (0.5 * INNER * STEP) * mass * slow_ref[...]
    v = v + (0.5 * STEP) * mass * fast_ref[...]
    x = x_ref[...] + STEP * v
    x_out[...] = x
    v_out[...] = v
    write_faces(swaps, x, None, index_ref, send_refs)


def pair_sums(receivers, sources, totals, slow_totals, sums, slow_sums):
    for it in range(len(receivers)):
        for st in range(len(sources)):
            closeness = dot(sources[st], receivers[it])
            high, low = two_parts(jnp.maximum(closeness, 0.0))
            sums[it] = sums[it] + (dot(totals[st], high) + dot(totals[st], low))
            if slow_totals is not None:
                ratio = SHORT_REACH / LONG_REACH
                wide = jnp.maximum(closeness * ratio + (1.0 - ratio), 0.0)
                high, low = two_parts(wide)
                lhs = slow_totals[it][st]
                slow_sums[it] = slow_sums[it] + (dot(lhs, high) + dot(lhs, low))


def short_from(u, sums):
    part = sums[0:8] + sums[8:16] + sums[16:24]
    return LEN * (u * part[3:4] - part)


def blocks(a, width=BLOCK):
    return [a[:, s : s + width] for s in range(0, a.shape[1], width)]


def tile_counts(own_ref, partner_ref, count_ref, n_tiles, swaps):
    slots = own_ref.shape[1]
    partner = partner_ref[...]
    own = own_ref[...]
    live = lax.broadcasted_iota(jnp.int32, (1, slots), 1) < count_ref[0]
    outside = partner - n_tiles
    axis = lax.shift_right_logical(outside, 2)
    side = lax.bitwise_and(lax.shift_right_logical(outside, 1), 1)
    within = lax.bitwise_and(outside, 1)
    place = jnp.full_like(partner, -1)
    for k, (ax, phase, _) in enumerate(swaps):
        even = lax.axis_index(AXES[ax]) % 2 == 0
        high = even if phase == 0 else jnp.logical_not(even)
        want = jnp.where(high, 1, 0)
        place = jnp.where((axis == ax) & (side == want), n_tiles + 2 * k + within, place)
    place = jnp.where(outside < 0, partner, place)
    own_hot = jnp.where((row_ids((8, slots)) == own) & live, 1.0, 0.0)
    place_hot = jnp.where(row_ids((32, slots)) == place, 1.0, 0.0)
    return lax.dot_general(own_hot, place_hot, (((1,), (1,)), ((), ())), preferred_element_type=F32)


def slow_matrices(u, charge, counts, first_tile):
    n = u.shape[1]
    ids = row_ids(u.shape)
    base = jnp.where(ids == 3, 1.0, u) * charge
    wide = []
    for t in range(8):
        per = [
            jnp.broadcast_to(counts[t : t + 1, first_tile + w : first_tile + w + 1], (1, LANES))
            for w in range(n // LANES)
        ]
        wide.append(jnp.concatenate(per, axis=1))
    out = []
    for it in range(4):
        parts = []
        for t in (2 * it, 2 * it + 1):
            parts.extend(split3(base * wide[t]))
        out.append(jnp.concatenate(parts, axis=0).astype(BF16))
    return out


def slow_from(u, charge, sums):
    low = sums[0:8] + sums[8:16] + sums[16:24]
    high = sums[24:32] + sums[32:40] + sums[40:48]
    part = jnp.concatenate([low[:, :LANES], high[:, LANES:]], axis=1)
    return (LONG_SCALE * LEN) * charge * (u * part[3:4] - part)


def own_kernel(swaps, first, last, *refs):
    refs = list(refs)
    x_ref, bonds_ref, bond_k_ref = refs[:3]
    refs = refs[3:]
    if not first:
        incidence = refs.pop(0)
    if last:
        charge_ref, own_ref, partner_ref, count_ref = refs[:4]
        refs = refs[4:]
    out_ref = refs.pop(0)
    if first:
        incidence = refs.pop(0)
    if last:
        slow_ref = refs.pop(0)
    x = x_ref[...]
    n = x.shape[1]
    tiles = lane_tiles(pad8(x))
    pulls = []
    for t in range(n // LANES):
        part = slice(t * LANES, (t + 1) * LANES)
        gap = gather_lanes(tiles, bonds_ref[0:1, part]) - gather_lanes(tiles, bonds_ref[1:2, part])
        pulls.append(bond_k_ref[:, part] * gap)
    pull = jnp.concatenate(pulls, axis=1)
    pull = jnp.concatenate(split3(pull), axis=0).astype(BF16)
    if first:
        for t in range(n // LANES):
            part = slice(t * LANES, (t + 1) * LANES)
            i = jnp.transpose(jnp.broadcast_to(bonds_ref[0:1, part], (LANES, LANES)))
            j = jnp.transpose(jnp.broadcast_to(bonds_ref[1:2, part], (LANES, LANES)))
            for s in range(n // LANES):
                atom = lax.broadcasted_iota(jnp.int32, (LANES, LANES), 1) + s * LANES
                hit = jnp.where(j == atom, 1.0, 0.0)
                hit = jnp.where(i == atom, hit - 1.0, hit)
                incidence[part, s * LANES : (s + 1) * LANES] = hit.astype(BF16)
    bonded = dot(pull, incidence[...])
    bonded = bonded[0:8] + bonded[8:16] + bonded[16:24]

    u = scaled(x, centre((8, n)))
    receivers = blocks(receiver_matrix(u))
    pair, total = source_matrices(u)
    sources = [jnp.transpose(p).astype(BF16) for p in blocks(pair)]
    totals = blocks(total)
    count = len(receivers)
    sums = [jnp.zeros((24, BLOCK), F32)] * count
    slow_totals = slow_sums = None
    if last:
        counts = tile_counts(own_ref, partner_ref, count_ref, n // LANES, swaps)
        per_source = [
            slow_matrices(b, q, counts, s * (BLOCK // LANES))
            for s, (b, q) in enumerate(zip(blocks(u), blocks(charge_ref[...])))
        ]
        slow_totals = [[per_source[s][it] for s in range(len(sources))] for it in range(count)]
        slow_sums = [jnp.zeros((48, BLOCK), F32)] * count
    pair_sums(receivers, sources, totals, slow_totals, sums, slow_sums)
    force = short_from(u, jnp.concatenate(sums, axis=1)) + bonded
    out_ref[...] = force[:3]
    if last:
        slow = [
            slow_from(b, q, s) for b, q, s in zip(blocks(u), blocks(charge_ref[...]), slow_sums)
        ]
        slow_ref[...] = jnp.concatenate(slow, axis=1)[:3]


def halo_kernel(swaps, last, send_charge, *refs):
    refs = list(refs)
    x_ref, v_ref, mass_ref, force_ref = refs[:4]
    refs = refs[4:]
    arrived = refs[: len(swaps)]
    refs = refs[len(swaps) :]
    if last:
        charge_ref, own_ref, partner_ref, count_ref, slow_ref, start_ref = refs[:6]
        moved_out, v_out, force_out, slow_out = refs[6:]
    else:
        index_ref = refs.pop(0)
        if send_charge:
            charge_ref = refs.pop(0)
        x_out, v_out = refs[:2]
        send_refs = refs[2:]
    x = x_ref[...]
    n = x.shape[1]
    u = scaled(x, centre((8, n)))
    receivers = blocks(receiver_matrix(u))
    count = len(receivers)
    mid = centre((8, BLOCK))
    sources, totals, slow_totals = [], [], [[] for _ in range(count)] if last else None
    if last:
        counts = tile_counts(own_ref, partner_ref, count_ref, n // LANES, swaps)
    for k, ((axis, phase, _), ref) in enumerate(zip(swaps, arrived)):
        place = lax.axis_index(AXES[axis])
        if phase == 0:
            valid = place >= 0
        else:
            valid = (place > 0) & (place < lax.axis_size(AXES[axis]) - 1)
        got = ref[...]
        there = jnp.where(valid, scaled(got, mid), 0.0)
        pair, total = source_matrices(there, valid)
        sources.append(jnp.transpose(pair).astype(BF16))
        totals.append(total)
        if last:
            per = slow_matrices(there, got[3:4], counts, n // LANES + k * (BLOCK // LANES))
            for it in range(count):
                slow_totals[it].append(per[it])
    sums = [jnp.zeros((24, BLOCK), F32)] * count
    slow_sums = [jnp.zeros((48, BLOCK), F32)] * count
    pair_sums(receivers, sources, totals, slow_totals, sums, slow_sums)
    mass = mass_ref[...]
    force = force_ref[...] + short_from(u, jnp.concatenate(sums, axis=1))[:3]
    v = v_ref[...] + (0.5 * STEP) * mass * force
    if last:
        slow = [
            slow_from(b, q, s) for b, q, s in zip(blocks(u), blocks(charge_ref[...]), slow_sums)
        ]
        slow = slow_ref[...] + jnp.concatenate(slow, axis=1)[:3]
        v_out[...] = v + (0.5 * INNER * STEP) * mass * slow
        moved_out[...] = x - start_ref[...]
        force_out[...] = force
        slow_out[...] = slow
    else:
        v = v + (0.5 * STEP) * mass * force
        x = x + STEP * v
        x_out[...] = x
        v_out[...] = v
        write_faces(swaps, x, charge_ref[...] if send_charge else None, index_ref, send_refs)


def call(kernel, outs, args, smem=(), flops=0):
    specs = [
        pl.BlockSpec(memory_space=pltpu.SMEM if i in smem else pltpu.VMEM) for i in range(len(args))
    ]
    return pl.pallas_call(
        kernel,
        out_shape=[jax.ShapeDtypeStruct(s, d) for s, d in outs],
        in_specs=specs,
        out_specs=[pl.BlockSpec(memory_space=pltpu.VMEM)] * len(outs),
        compiler_params=pltpu.CompilerParams(vmem_limit_bytes=24 * 1024 * 1024),
        cost_estimate=pl.CostEstimate(flops=flops, bytes_accessed=100000, transcendentals=0),
    )(*args)


def on_device(
    swaps,
    positions,
    velocities,
    inv_mass,
    charge,
    fast_force,
    slow_force,
    bonds,
    bond_k,
    halo_index,
    pair_own,
    pair_partner,
    pair_count,
):
    n = positions.shape[1]
    width = halo_index.shape[1]
    mass = inv_mass.reshape(1, n)
    charge = charge.reshape(1, n)
    bond_k = bond_k.reshape(1, -1)
    own = pair_own.reshape(1, -1)
    partner = pair_partner.reshape(1, -1)
    vec = ((3, n), F32)
    sends = [((4, width), F32)] * len(swaps)
    x, v, *faces = call(
        functools.partial(start_kernel, swaps),
        [vec, vec] + sends,
        [positions, velocities, mass, fast_force, slow_force, halo_index],
    )
    incidence = None
    for turn in range(INNER):
        first, last = turn == 0, turn == INNER - 1
        arrived = [lax.ppermute(f, AXES, perm) for f, (_, _, perm) in zip(faces, swaps)]
        outs = [vec]
        args = [x, bonds, bond_k]
        smem = ()
        if first:
            outs.append(((bonds.shape[1], n), BF16))
        else:
            args.append(incidence)
        if last:
            args += [charge, own, partner, pair_count]
            smem = (len(args) - 1,)
            outs.append(vec)
        got = call(
            functools.partial(own_kernel, swaps, first, last), outs, args, smem, flops=2 * 10**9
        )
        force = got[0]
        if first:
            incidence = got[1]
        args = [x, v, mass, force] + arrived
        if last:
            args += [charge, own, partner, pair_count, got[-1], positions]
            moved, v, force, slow = call(
                functools.partial(halo_kernel, swaps, True, False),
                [vec] * 4,
                args,
                (len(args) - 3,),
                flops=10**9,
            )
            return moved, v, force, slow
        send_charge = turn == INNER - 2
        args.append(halo_index)
        if send_charge:
            args.append(charge)
        x, v, *faces = call(
            functools.partial(halo_kernel, swaps, False, send_charge),
            [vec, vec] + sends,
            args,
            flops=10**9,
        )


def solution(mesh):
    rows = P(None, AXES)
    flat = P(AXES)
    swaps = matchings([mesh.shape[ax] for ax in AXES])
    return jax.shard_map(
        functools.partial(on_device, swaps),
        mesh=mesh,
        in_specs=(rows, rows, flat, flat, rows, rows, rows, flat, rows, flat, flat, flat),
        out_specs=(rows, rows, rows, rows),
        check_vma=False,
    )
```

profile of v0, /device:TPU:0, one launch (start us, length us, event | category | flops | bytes accessed | tf_op | source)
XLA Modules:
  0.0 50.9 jit_solution(9102497245363314526)
XLA Ops:
  0.6 0.7 %copy-done = f32[3,1024]{1,0:T(4,128)S(1)} copy-done((f32[3,1024]{1,0:T(4,128)S(1)}, f32[3,1024]{1,0:T(4,128)}, u32[]{:S(2)}) %copy-start) | copy-done | bytes 12312
  1.4 0.7 %copy-done.1 = f32[3,1024]{1,0:T(4,128)S(1)} copy-done((f32[3,1024]{1,0:T(4,128)S(1)}, f32[3,1024]{1,0:T(4,128)}, u32[]{:S(2)}) %copy-start.1) | copy-done | bytes 12312
  2.1 0.7 %copy-done.2 = f32[3,1024]{1,0:T(4,128)S(1)} copy-done((f32[3,1024]{1,0:T(4,128)S(1)}, f32[3,1024]{1,0:T(4,128)}, u32[]{:S(2)}) %copy-start.2) | copy-done | bytes 12312
  2.8 0.7 %copy-done.3 = f32[3,1024]{1,0:T(4,128)S(1)} copy-done((f32[3,1024]{1,0:T(4,128)S(1)}, f32[3,1024]{1,0:T(4,128)}, u32[]{:S(2)}) %copy-start.3) | copy-done | bytes 12312
  3.5 0.7 %copy-done.5 = s32[6,256]{1,0:T(8,128)S(1)} copy-done((s32[6,256]{1,0:T(8,128)S(1)}, s32[6,256]{1,0:T(8,128)}, u32[]{:S(2)}) %copy-start.5) | copy-done | bytes 6168
  5.1 3.1 %collective-permute-start = (f32[4,256]{1,0:T(4,128)S(1)}, f32[4,256]{1,0:T(4,128)S(1)}, u32[]{:S(2)}, u32[]{:S(2)}) collective-permute-start(f32[4,256]{1,0:T(4,128)S(1)} %get-tuple-element.39), channel_id=1, source_target_pairs={{0,1},{1,0},{2,3},{3,2},{4,5},{5,4},{6,7},{7,6},{8,9},{9,8},{10,11... | collective-permute-start | bytes 12296 | tf_op jit(solution)/shard_map/ppermute | solution.py:402
  8.2 1.5 %collective-permute-start.2 = (f32[4,256]{1,0:T(4,128)S(1)}, f32[4,256]{1,0:T(4,128)S(1)}, u32[]{:S(2)}, u32[]{:S(2)}) collective-permute-start(f32[4,256]{1,0:T(4,128)S(1)} %get-tuple-element.41), channel_id=1, source_target_pairs={{0,16},{1,17},{2,18},{3,19},{4,20},{5,21},{6,22},{7,23},{8,24},{9,... | collective-permute-start | bytes 12296 | tf_op jit(solution)/shard_map/ppermute | solution.py:402
  10.5 0.7 %copy-done.9 = s32[2,1024]{1,0:T(2,128)S(1)} copy-done((s32[2,1024]{1,0:T(2,128)S(1)}, s32[2,1024]{1,0:T(2,128)}, u32[]{:S(2)}) %copy-start.9) | copy-done | bytes 8216
  11.9 3.0 %shard_map.148 = (f32[3,1024]{1,0:T(4,128)S(1)}, bf16[1024,1024]{1,0:T(8,128)(2,1)S(1)}) custom-call(f32[3,1024]{1,0:T(4,128)S(1)} %get-tuple-element.36.refs_0_, s32[2,1024]{1,0:T(2,128)S(1)} %copy-done.9, f32[1,1024]{1,0:T(1,128)S(1)} %bitcast.10), custom_call_target="tpu_custom_call" | custom-call | flops 2000000000 | bytes 100000 | tf_op jit(solution)/shard_map/pallas_call | solution.py:360
  15.5 1.9 %shard_map.149 = (f32[3,1024]{1,0:T(4,128)S(1)}, f32[3,1024]{1,0:T(4,128)S(1)}, f32[4,256]{1,0:T(4,128)S(1)}, f32[4,256]{1,0:T(4,128)S(1)}, f32[4,256]{1,0:T(4,1...) custom-call(f32[3,1024]{1,0:T(4,128)S(1)} %get-tuple-element.36.refs_0_, f32[3,1024]{1,0:T(4,128)S(1)} %get-tuple-element.37.refs_1_, ...), custom_call_target="tpu_custom_call" | custom-call | flops 1000000000 | bytes 100000 | tf_op jit(solution)/shard_map/pallas_call | solution.py:360
  17.4 3.0 %collective-permute-start.5 = (f32[4,256]{1,0:T(4,128)S(1)}, f32[4,256]{1,0:T(4,128)S(1)}, u32[]{:S(2)}, u32[]{:S(2)}) collective-permute-start(f32[4,256]{1,0:T(4,128)S(1)} %get-tuple-element.47), channel_id=1, source_target_pairs={{0,1},{1,0},{2,3},{3,2},{4,5},{5,4},{6,7},{7,6},{8,9},{9,8},{10,11... | collective-permute-start | bytes 12296 | tf_op jit(solution)/shard_map/ppermute | solution.py:402
  20.4 0.8 %collective-permute-start.6 = (f32[4,256]{1,0:T(4,128)S(1)}, f32[4,256]{1,0:T(4,128)S(1)}, u32[]{:S(2)}, u32[]{:S(2)}) collective-permute-start(f32[4,256]{1,0:T(4,128)S(1)} %get-tuple-element.48), channel_id=1, source_target_pairs={{0,4},{1,2},{2,1},{3,7},{4,0},{5,6},{6,5},{7,3},{8,12},{9,10},{10,... | collective-permute-start | bytes 12296 | tf_op jit(solution)/shard_map/ppermute | solution.py:402
  22.2 1.1 %collective-permute-start.9 = (f32[4,256]{1,0:T(4,128)S(1)}, f32[4,256]{1,0:T(4,128)S(1)}, u32[]{:S(2)}, u32[]{:S(2)}) collective-permute-start(f32[4,256]{1,0:T(4,128)S(1)} %get-tuple-element.51), channel_id=1, source_target_pairs={{0,16},{1,17},{2,18},{3,19},{4,8},{5,9},{6,10},{7,11},{8,4},{9,5},... | collective-permute-start | bytes 12296 | tf_op jit(solution)/shard_map/ppermute | solution.py:402
  23.3 2.1 %shard_map.150.refs_3_ = f32[3,1024]{1,0:T(4,128)S(1)} custom-call(f32[3,1024]{1,0:T(4,128)S(1)} %get-tuple-element.44.refs_0_, s32[2,1024]{1,0:T(2,128)S(1)} %copy-done.9, f32[1,1024]{1,0:T(1,128)S(1)} %bitcast.11, bf16[1024,1024]{1,0:T(8,128)(2,1)S(1)} %get-tuple-element.46.refs_3_), custom_call_target="tpu_custom_call" | custom-call | flops 2000000000 | bytes 100000 | tf_op jit(solution)/shard_map/pallas_call | solution.py:360
  25.8 1.9 %shard_map.151 = (f32[3,1024]{1,0:T(4,128)S(1)}, f32[3,1024]{1,0:T(4,128)S(1)}, f32[4,256]{1,0:T(4,128)S(1)}, f32[4,256]{1,0:T(4,128)S(1)}, f32[4,256]{1,0:T(4,1...) custom-call(f32[3,1024]{1,0:T(4,128)S(1)} %get-tuple-element.44.refs_0_, f32[3,1024]{1,0:T(4,128)S(1)} %get-tuple-element.45.refs_1_, ...), custom_call_target="tpu_custom_call" | custom-call | flops 1000000000 | bytes 100000 | tf_op jit(solution)/shard_map/pallas_call | solution.py:360
  28.2 0.9 %collective-permute-start.12 = (f32[4,256]{1,0:T(4,128)S(1)}, f32[4,256]{1,0:T(4,128)S(1)}, u32[]{:S(2)}, u32[]{:S(2)}) collective-permute-start(f32[4,256]{1,0:T(4,128)S(1)} %get-tuple-element.56), channel_id=1, source_target_pairs={{0,16},{1,17},{2,18},{3,19},{4,20},{5,21},{6,22},{7,23},{8,24},{9,... | collective-permute-start | bytes 12296 | tf_op jit(solution)/shard_map/ppermute | solution.py:402
  29.2 1.2 %collective-permute-start.14 = (f32[4,256]{1,0:T(4,128)S(1)}, f32[4,256]{1,0:T(4,128)S(1)}, u32[]{:S(2)}, u32[]{:S(2)}) collective-permute-start(f32[4,256]{1,0:T(4,128)S(1)} %get-tuple-element.58), channel_id=1, source_target_pairs={{0,16},{1,17},{2,18},{3,19},{4,8},{5,9},{6,10},{7,11},{8,4},{9,5},... | collective-permute-start | bytes 12296 | tf_op jit(solution)/shard_map/ppermute | solution.py:402
  30.4 2.1 %shard_map.152.refs_3_ = f32[3,1024]{1,0:T(4,128)S(1)} custom-call(f32[3,1024]{1,0:T(4,128)S(1)} %get-tuple-element.52.refs_0_, s32[2,1024]{1,0:T(2,128)S(1)} %copy-done.9, f32[1,1024]{1,0:T(1,128)S(1)} %bitcast.12, bf16[1024,1024]{1,0:T(8,128)(2,1)S(1)} %get-tuple-element.46.refs_3_), custom_call_target="tpu_custom_call" | custom-call | flops 2000000000 | bytes 100000 | tf_op jit(solution)/shard_map/pallas_call | solution.py:360
  32.8 2.1 %shard_map.153 = (f32[3,1024]{1,0:T(4,128)S(1)}, f32[3,1024]{1,0:T(4,128)S(1)}, f32[4,256]{1,0:T(4,128)S(1)}, f32[4,256]{1,0:T(4,128)S(1)}, f32[4,256]{1,0:T(4,1...) custom-call(f32[3,1024]{1,0:T(4,128)S(1)} %get-tuple-element.52.refs_0_, f32[3,1024]{1,0:T(4,128)S(1)} %get-tuple-element.53.refs_1_, ...), custom_call_target="tpu_custom_call" | custom-call | flops 1000000000 | bytes 100000 | tf_op jit(solution)/shard_map/pallas_call | solution.py:360
  34.9 1.7 %collective-permute-start.15 = (f32[4,256]{1,0:T(4,128)S(1)}, f32[4,256]{1,0:T(4,128)S(1)}, u32[]{:S(2)}, u32[]{:S(2)}) collective-permute-start(f32[4,256]{1,0:T(4,128)S(1)} %get-tuple-element.62), channel_id=1, source_target_pairs={{0,1},{1,0},{2,3},{3,2},{4,5},{5,4},{6,7},{7,6},{8,9},{9,8},{10,11... | collective-permute-start | bytes 12296 | tf_op jit(solution)/shard_map/ppermute | solution.py:402
  36.6 0.9 %collective-permute-start.17 = (f32[4,256]{1,0:T(4,128)S(1)}, f32[4,256]{1,0:T(4,128)S(1)}, u32[]{:S(2)}, u32[]{:S(2)}) collective-permute-start(f32[4,256]{1,0:T(4,128)S(1)} %get-tuple-element.64), channel_id=1, source_target_pairs={{0,16},{1,17},{2,18},{3,19},{4,20},{5,21},{6,22},{7,23},{8,24},{9,... | collective-permute-start | bytes 12296 | tf_op jit(solution)/shard_map/ppermute | solution.py:402
  37.7 1.1 %collective-permute-start.19 = (f32[4,256]{1,0:T(4,128)S(1)}, f32[4,256]{1,0:T(4,128)S(1)}, u32[]{:S(2)}, u32[]{:S(2)}) collective-permute-start(f32[4,256]{1,0:T(4,128)S(1)} %get-tuple-element.66), channel_id=1, source_target_pairs={{0,16},{1,17},{2,18},{3,19},{4,8},{5,9},{6,10},{7,11},{8,4},{9,5},... | collective-permute-start | bytes 12296 | tf_op jit(solution)/shard_map/ppermute | solution.py:402
  38.9 5.3 %shard_map.154 = (f32[3,1024]{1,0:T(4,128)S(1)}, f32[3,1024]{1,0:T(4,128)S(1)}) custom-call(f32[3,1024]{1,0:T(4,128)S(1)} %get-tuple-element.59.refs_0_, s32[2,1024]{1,0:T(2,128)S(1)} %copy-done.9, f32[1,1024]{1,0:T(1,128)S(1)} %bitcast.13, bf16[1024,1024]{1,0:T(8,128)(2,1)S(1)} %get-tuple-element.46.refs_3_, f32[1,1024]{1,0:T(1,128)S(1)} %bitcast.15, ...), custom_call_target="tpu_custom_call" | custom-call | flops 2000000000 | bytes 100000 | tf_op jit(solution)/shard_map/pallas_call | solution.py:360
  44.3 6.6 %shard_map.155 = (f32[3,1024]{1,0:T(4,128)}, f32[3,1024]{1,0:T(4,128)}, f32[3,1024]{1,0:T(4,128)}, f32[3,1024]{1,0:T(4,128)}) custom-call(f32[3,1024]{1,0:T(4,128)S(1)} %get-tuple-element.59.refs_0_, f32[3,1024]{1,0:T(4,128)S(1)} %get-tuple-element.60.refs_1_, f32[1,1024]{1,0:T(1,128)S(1)} %bitcast.9, f32[3,1024]{1,0:T(4,128)S(1)} %get-tuple-element.61.refs_3_, ...), custom_call_target="tpu_custom_call" | custom-call | flops 1000000000 | bytes 100000 | tf_op jit(solution)/shard_map/pallas_call | solution.py:360
  (55 shorter events, 4.9 us)
Async XLA Ops:
  5.1 10.4 %collective-permute-start = (f32[4,256]{1,0:T(4,128)S(1)}, f32[4,256]{1,0:T(4,128)S(1)}, u32[]{:S(2)}, u32[]{:S(2)}) collective-permute-start(f32[4,256]{1,0:T(4,128)S(1)} %get-tuple-element.39), channel_id=1, source_target_pairs={{0,1},{1,0},{2,3},{3,2},{4,5},{5,4},{6,7},{7,6},{8,9},{9,8},{10,11... | collective-permute-start | bytes 12296 | tf_op jit(solution)/shard_map/ppermute | solution.py:402
  8.2 7.3 %collective-permute-start.1 = (f32[4,256]{1,0:T(4,128)S(1)}, f32[4,256]{1,0:T(4,128)S(1)}, u32[]{:S(2)}, u32[]{:S(2)}) collective-permute-start(f32[4,256]{1,0:T(4,128)S(1)} %get-tuple-element.40), channel_id=1, source_target_pairs={{0,4},{1,2},{2,1},{3,7},{4,0},{5,6},{6,5},{7,3},{8,12},{9,10},{10,... | collective-permute-start | bytes 12296 | tf_op jit(solution)/shard_map/ppermute | solution.py:402
  8.2 7.3 %collective-permute-start.2 = (f32[4,256]{1,0:T(4,128)S(1)}, f32[4,256]{1,0:T(4,128)S(1)}, u32[]{:S(2)}, u32[]{:S(2)}) collective-permute-start(f32[4,256]{1,0:T(4,128)S(1)} %get-tuple-element.41), channel_id=1, source_target_pairs={{0,16},{1,17},{2,18},{3,19},{4,20},{5,21},{6,22},{7,23},{8,24},{9,... | collective-permute-start | bytes 12296 | tf_op jit(solution)/shard_map/ppermute | solution.py:402
  9.7 5.8 %collective-permute-start.3 = (f32[4,256]{1,0:T(4,128)S(1)}, f32[4,256]{1,0:T(4,128)S(1)}, u32[]{:S(2)}, u32[]{:S(2)}) collective-permute-start(f32[4,256]{1,0:T(4,128)S(1)} %get-tuple-element.42), channel_id=1, source_target_pairs={{0,4},{1,5},{2,6},{3,7},{4,0},{5,1},{6,2},{7,3},{8,12},{9,13},{10,... | collective-permute-start | bytes 12296 | tf_op jit(solution)/shard_map/ppermute | solution.py:402
  9.9 5.6 %collective-permute-start.4 = (f32[4,256]{1,0:T(4,128)S(1)}, f32[4,256]{1,0:T(4,128)S(1)}, u32[]{:S(2)}, u32[]{:S(2)}) collective-permute-start(f32[4,256]{1,0:T(4,128)S(1)} %get-tuple-element.43), channel_id=1, source_target_pairs={{0,16},{1,17},{2,18},{3,19},{4,8},{5,9},{6,10},{7,11},{8,4},{9,5},... | collective-permute-start | bytes 12296 | tf_op jit(solution)/shard_map/ppermute | solution.py:402
  17.4 7.9 %collective-permute-start.5 = (f32[4,256]{1,0:T(4,128)S(1)}, f32[4,256]{1,0:T(4,128)S(1)}, u32[]{:S(2)}, u32[]{:S(2)}) collective-permute-start(f32[4,256]{1,0:T(4,128)S(1)} %get-tuple-element.47), channel_id=1, source_target_pairs={{0,1},{1,0},{2,3},{3,2},{4,5},{5,4},{6,7},{7,6},{8,9},{9,8},{10,11... | collective-permute-start | bytes 12296 | tf_op jit(solution)/shard_map/ppermute | solution.py:402
  20.4 4.9 %collective-permute-start.6 = (f32[4,256]{1,0:T(4,128)S(1)}, f32[4,256]{1,0:T(4,128)S(1)}, u32[]{:S(2)}, u32[]{:S(2)}) collective-permute-start(f32[4,256]{1,0:T(4,128)S(1)} %get-tuple-element.48), channel_id=1, source_target_pairs={{0,4},{1,2},{2,1},{3,7},{4,0},{5,6},{6,5},{7,3},{8,12},{9,10},{10,... | collective-permute-start | bytes 12296 | tf_op jit(solution)/shard_map/ppermute | solution.py:402
  21.3 4.1 %collective-permute-start.7 = (f32[4,256]{1,0:T(4,128)S(1)}, f32[4,256]{1,0:T(4,128)S(1)}, u32[]{:S(2)}, u32[]{:S(2)}) collective-permute-start(f32[4,256]{1,0:T(4,128)S(1)} %get-tuple-element.49), channel_id=1, source_target_pairs={{0,16},{1,17},{2,18},{3,19},{4,20},{5,21},{6,22},{7,23},{8,24},{9,... | collective-permute-start | bytes 12296 | tf_op jit(solution)/shard_map/ppermute | solution.py:402
  21.9 3.5 %collective-permute-start.8 = (f32[4,256]{1,0:T(4,128)S(1)}, f32[4,256]{1,0:T(4,128)S(1)}, u32[]{:S(2)}, u32[]{:S(2)}) collective-permute-start(f32[4,256]{1,0:T(4,128)S(1)} %get-tuple-element.50), channel_id=1, source_target_pairs={{0,4},{1,5},{2,6},{3,7},{4,0},{5,1},{6,2},{7,3},{8,12},{9,13},{10,... | collective-permute-start | bytes 12296 | tf_op jit(solution)/shard_map/ppermute | solution.py:402
  22.2 3.6 %collective-permute-start.9 = (f32[4,256]{1,0:T(4,128)S(1)}, f32[4,256]{1,0:T(4,128)S(1)}, u32[]{:S(2)}, u32[]{:S(2)}) collective-permute-start(f32[4,256]{1,0:T(4,128)S(1)} %get-tuple-element.51), channel_id=1, source_target_pairs={{0,16},{1,17},{2,18},{3,19},{4,8},{5,9},{6,10},{7,11},{8,4},{9,5},... | collective-permute-start | bytes 12296 | tf_op jit(solution)/shard_map/ppermute | solution.py:402
  27.6 4.9 %collective-permute-start.10 = (f32[4,256]{1,0:T(4,128)S(1)}, f32[4,256]{1,0:T(4,128)S(1)}, u32[]{:S(2)}, u32[]{:S(2)}) collective-permute-start(f32[4,256]{1,0:T(4,128)S(1)} %get-tuple-element.54), channel_id=1, source_target_pairs={{0,1},{1,0},{2,3},{3,2},{4,5},{5,4},{6,7},{7,6},{8,9},{9,8},{10,11... | collective-permute-start | bytes 12296 | tf_op jit(solution)/shard_map/ppermute | solution.py:402
  28.2 4.4 %collective-permute-start.11 = (f32[4,256]{1,0:T(4,128)S(1)}, f32[4,256]{1,0:T(4,128)S(1)}, u32[]{:S(2)}, u32[]{:S(2)}) collective-permute-start(f32[4,256]{1,0:T(4,128)S(1)} %get-tuple-element.55), channel_id=1, source_target_pairs={{0,4},{1,2},{2,1},{3,7},{4,0},{5,6},{6,5},{7,3},{8,12},{9,10},{10,... | collective-permute-start | bytes 12296 | tf_op jit(solution)/shard_map/ppermute | solution.py:402
  28.2 4.4 %collective-permute-start.12 = (f32[4,256]{1,0:T(4,128)S(1)}, f32[4,256]{1,0:T(4,128)S(1)}, u32[]{:S(2)}, u32[]{:S(2)}) collective-permute-start(f32[4,256]{1,0:T(4,128)S(1)} %get-tuple-element.56), channel_id=1, source_target_pairs={{0,16},{1,17},{2,18},{3,19},{4,20},{5,21},{6,22},{7,23},{8,24},{9,... | collective-permute-start | bytes 12296 | tf_op jit(solution)/shard_map/ppermute | solution.py:402
  29.0 3.5 %collective-permute-start.13 = (f32[4,256]{1,0:T(4,128)S(1)}, f32[4,256]{1,0:T(4,128)S(1)}, u32[]{:S(2)}, u32[]{:S(2)}) collective-permute-start(f32[4,256]{1,0:T(4,128)S(1)} %get-tuple-element.57), channel_id=1, source_target_pairs={{0,4},{1,5},{2,6},{3,7},{4,0},{5,1},{6,2},{7,3},{8,12},{9,13},{10,... | collective-permute-start | bytes 12296 | tf_op jit(solution)/shard_map/ppermute | solution.py:402
  29.2 3.6 %collective-permute-start.14 = (f32[4,256]{1,0:T(4,128)S(1)}, f32[4,256]{1,0:T(4,128)S(1)}, u32[]{:S(2)}, u32[]{:S(2)}) collective-permute-start(f32[4,256]{1,0:T(4,128)S(1)} %get-tuple-element.58), channel_id=1, source_target_pairs={{0,16},{1,17},{2,18},{3,19},{4,8},{5,9},{6,10},{7,11},{8,4},{9,5},... | collective-permute-start | bytes 12296 | tf_op jit(solution)/shard_map/ppermute | solution.py:402
  32.5 6.4 %copy-start.11 = (f32[1024]{0:T(1024)S(1)}, f32[1024]{0:T(1024)}, u32[]{:S(2)}) copy-start(f32[1024]{0:T(1024)} %param.19) | copy-start | bytes 12292
  32.5 6.4 %copy-start.13 = (s32[96]{0:T(128)S(1)}, s32[96]{0:T(128)}, u32[]{:S(2)}) copy-start(s32[96]{0:T(128)} %param.21) | copy-start | bytes 1156
  32.5 6.4 %copy-start.14 = (s32[96]{0:T(128)S(1)}, s32[96]{0:T(128)}, u32[]{:S(2)}) copy-start(s32[96]{0:T(128)} %param.22) | copy-start | bytes 1156
  34.9 9.3 %collective-permute-start.15 = (f32[4,256]{1,0:T(4,128)S(1)}, f32[4,256]{1,0:T(4,128)S(1)}, u32[]{:S(2)}, u32[]{:S(2)}) collective-permute-start(f32[4,256]{1,0:T(4,128)S(1)} %get-tuple-element.62), channel_id=1, source_target_pairs={{0,1},{1,0},{2,3},{3,2},{4,5},{5,4},{6,7},{7,6},{8,9},{9,8},{10,11... | collective-permute-start | bytes 12296 | tf_op jit(solution)/shard_map/ppermute | solution.py:402
  36.6 7.6 %collective-permute-start.16 = (f32[4,256]{1,0:T(4,128)S(1)}, f32[4,256]{1,0:T(4,128)S(1)}, u32[]{:S(2)}, u32[]{:S(2)}) collective-permute-start(f32[4,256]{1,0:T(4,128)S(1)} %get-tuple-element.63), channel_id=1, source_target_pairs={{0,4},{1,2},{2,1},{3,7},{4,0},{5,6},{6,5},{7,3},{8,12},{9,10},{10,... | collective-permute-start | bytes 12296 | tf_op jit(solution)/shard_map/ppermute | solution.py:402
  36.6 7.6 %collective-permute-start.17 = (f32[4,256]{1,0:T(4,128)S(1)}, f32[4,256]{1,0:T(4,128)S(1)}, u32[]{:S(2)}, u32[]{:S(2)}) collective-permute-start(f32[4,256]{1,0:T(4,128)S(1)} %get-tuple-element.64), channel_id=1, source_target_pairs={{0,16},{1,17},{2,18},{3,19},{4,20},{5,21},{6,22},{7,23},{8,24},{9,... | collective-permute-start | bytes 12296 | tf_op jit(solution)/shard_map/ppermute | solution.py:402
  37.5 6.8 %collective-permute-start.18 = (f32[4,256]{1,0:T(4,128)S(1)}, f32[4,256]{1,0:T(4,128)S(1)}, u32[]{:S(2)}, u32[]{:S(2)}) collective-permute-start(f32[4,256]{1,0:T(4,128)S(1)} %get-tuple-element.65), channel_id=1, source_target_pairs={{0,4},{1,5},{2,6},{3,7},{4,0},{5,1},{6,2},{7,3},{8,12},{9,13},{10,... | collective-permute-start | bytes 12296 | tf_op jit(solution)/shard_map/ppermute | solution.py:402
  37.7 6.5 %collective-permute-start.19 = (f32[4,256]{1,0:T(4,128)S(1)}, f32[4,256]{1,0:T(4,128)S(1)}, u32[]{:S(2)}, u32[]{:S(2)}) collective-permute-start(f32[4,256]{1,0:T(4,128)S(1)} %get-tuple-element.66), channel_id=1, source_target_pairs={{0,16},{1,17},{2,18},{3,19},{4,8},{5,9},{6,10},{7,11},{8,4},{9,5},... | collective-permute-start | bytes 12296 | tf_op jit(solution)/shard_map/ppermute | solution.py:402
  38.9 5.4 %copy-start.4 = (f32[3,1024]{1,0:T(4,128)S(1)}, f32[3,1024]{1,0:T(4,128)}, u32[]{:S(2)}) copy-start(f32[3,1024]{1,0:T(4,128)} %refs_14_.1) | copy-start | bytes 36868
  (11 other events, 15.4 us)
where the time goes:
time: 51.6 us; the launch traced here: 50.9 us
  Pallas kernels  25.1 us (49%)
  starting transfers between devices  17.9 us (35%)
  local copies, waits for them, and re-layouts  5.66 us (11%)
  between operations  1.56 us (3%)
  waiting for transfers between devices  0.69 us (1%)
    pallas_call x9, Pallas kernels, call(): pl.pallas_call(kernel, out_shape=[jax.ShapeDtypeStruct(s, d) for s, d in...  25.1 us
    ppermute x20, starting transfers between devices, on_device(): lax.ppermute(f, AXES, perm)  17.9 us
    unnamed x30, local copies, waits for them, and re-layouts  5.66 us
  transfers between devices with their start and end apart: 20, of which 2 were waited for; matrix products, arithmetic and copies ran while one was open for 0% of the time, Pallas kernels for 24%

commit v1 on v0

v1 whole, which is shorter than its diff:
```python
import functools

import jax
import jax.numpy as jnp
from jax import lax
from jax.experimental import pallas as pl
from jax.experimental.pallas import tpu as pltpu
from jax.sharding import PartitionSpec as P

AXES = ("gx", "gy", "gz")
INNER = 4
STEP = 0.1
LONG_SCALE = 0.5
SIDE = 4.0
SHORT_UNIT = 0.8
LONG_UNIT = 1.2
LANES = 128
BLOCK = 256
FAR = -1.0e6

N_START = 12
F32 = jnp.float32
BF16 = jnp.bfloat16


def matchings(sizes):
    nx, ny, nz = sizes
    assert nx % 2 == 0 and ny % 2 == 0 and nz % 2 == 0
    swaps = []
    for axis in (2, 0, 1):
        for phase in range(1 if sizes[axis] == 2 else 2):
            perm = []
            for a in range(nx):
                for b in range(ny):
                    for c in range(nz):
                        place = [a, b, c]
                        p = place[axis]
                        partner = p ^ 1 if phase == 0 else (p + 1 if p % 2 else p - 1)
                        if 0 <= partner < sizes[axis]:
                            place[axis] = partner
                        else:
                            other = 0 if axis == 1 else 1
                            place[other] ^= 1
                        perm.append(
                            ((a * ny + b) * nz + c, (place[0] * ny + place[1]) * nz + place[2])
                        )
            swaps.append((axis, phase, perm))
    return swaps


def rounded(a):
    return a.astype(BF16).astype(F32)


def split3(a):
    high = rounded(a)
    rest = a - high
    mid = rounded(rest)
    return high, mid, rounded(rest - mid)


def row_ids(shape):
    return lax.broadcasted_iota(jnp.int32, shape, 0)


def pick_rows(rows, shape):
    ids = row_ids(shape)
    out = jnp.zeros(shape, F32)
    for s, r in enumerate(rows):
        out = jnp.where(ids == s, r, out)
    return out


def centre(shape):
    parts = [lax.axis_index(ax).astype(F32) * SIDE + 0.5 * SIDE for ax in AXES]
    return pick_rows(parts, shape)


def scaled(x, mid, unit):
    n = x.shape[1]
    full = jnp.concatenate([x[:3], jnp.zeros((5, n), F32)], axis=0)
    return (full - mid) * (1.0 / unit)


def receiver_matrix(u):
    h, m, l = split3(u)
    norm = 1.0 - jnp.sum(u * u, axis=0, keepdims=True)
    a, b, c = split3(norm)
    h, m, l = 2.0 * h, 2.0 * m, 2.0 * l
    one = jnp.ones_like(norm)
    tail = pick_rows([a, b, c, one, one, one], u.shape)
    return jnp.concatenate([h, h, h, m, m, l, tail, jnp.zeros_like(u)], axis=0).astype(BF16)


def source_matrices(u, valid=None):
    h, m, l = split3(u)
    norm = -jnp.sum(u * u, axis=0, keepdims=True)
    if valid is not None:
        norm = jnp.where(valid, norm, FAR)
    a, b, c = split3(norm)
    one = jnp.ones_like(norm)
    tail = pick_rows([one, one, one, a, b, c], u.shape)
    pair = jnp.concatenate([h, m, l, h, m, h, tail, jnp.zeros_like(u)], axis=0)
    ids = row_ids(u.shape)
    total = jnp.concatenate([jnp.where(ids == 3, 1.0, h), m, l], axis=0)
    return pair, total


def dot(a, b):
    return jnp.dot(a, b, preferred_element_type=F32)


def two_parts(w):
    return w, w - rounded(w)


def gather_lanes(sources, index):
    index = jnp.broadcast_to(index, (8, LANES))
    tile = lax.shift_right_logical(index, 7)
    lane = lax.bitwise_and(index, LANES - 1)
    out = jnp.zeros((8, LANES), F32)
    for r, src in enumerate(sources):
        out = jnp.where(tile == r, jnp.take_along_axis(src, lane, axis=1), out)
    return out


def lane_tiles(a):
    return [a[:, r * LANES : (r + 1) * LANES] for r in range(a.shape[1] // LANES)]


def pad8(x):
    return jnp.concatenate([x, jnp.zeros((8 - x.shape[0], x.shape[1]), F32)], axis=0)


def write_faces(swaps, x, charge, index_ref, send_refs):
    rows = [x] if charge is None else [x, charge]
    tiles = lane_tiles(pad8(jnp.concatenate(rows, axis=0)))
    for (axis, phase, _), ref in zip(swaps, send_refs):
        even = lax.axis_index(AXES[axis]) % 2 == 0
        high = even if phase == 0 else jnp.logical_not(even)
        index = jnp.where(high, index_ref[2 * axis + 1 : 2 * axis + 2, :], index_ref[2 * axis : 2 * axis + 1, :])
        for w in range(index.shape[1] // LANES):
            part = slice(w * LANES, (w + 1) * LANES)
            ref[:, part] = gather_lanes(tiles, index[:, part])[:4]


def start_kernel(swaps, *refs):
    sources, refs = refs[:N_START], refs[N_START:]
    x_ref, mass_ref, index_ref = refs[:3]
    kept, refs = refs[3 : N_START - 3], refs[N_START - 3 :]
    x_out, v_out = refs[:2]
    send_refs, (v_ref, fast_ref, slow_ref, sems) = refs[2 : 2 + len(swaps)], refs[2 + len(swaps) :]
    kept = [x_ref, mass_ref, index_ref, v_ref, fast_ref, slow_ref, *kept]
    copies = [
        pltpu.make_async_copy(src, dst, sems.at[k]) for k, (src, dst) in enumerate(zip(sources, kept))
    ]
    for c in copies:
        c.start()
    for c in copies[:6]:
        c.wait()
    mass = mass_ref[...]
    v = v_ref[...] + (0.5 * INNER * STEP) * mass * slow_ref[...]
    v = v + (0.5 * STEP) * mass * fast_ref[...]
    x = x_ref[...] + STEP * v
    x_out[...] = x
    v_out[...] = v
    write_faces(swaps, x, None, index_ref, send_refs)
    for c in copies[6:]:
        c.wait()


def pair_sums(receivers, sources, totals, fold=None):
    sums = []
    for it in range(len(receivers)):
        out = None
        for st in range(len(sources)):
            closeness = dot(sources[st], receivers[it])
            high, low = two_parts(jnp.maximum(closeness, 0.0))
            part = dot(totals[st], high) + dot(totals[st], low)
            if fold is not None:
                part = fold(it, st, part)
            out = part if out is None else out + part
        sums.append(out)
    return sums


def short_from(u, sums):
    part = sums[0:8] + sums[8:16] + sums[16:24]
    return SHORT_UNIT * (u * part[3:4] - part)


def blocks(a, width=BLOCK):
    return [a[:, s : s + width] for s in range(0, a.shape[1], width)]


def tile_counts(own_ref, partner_ref, count_ref, n_tiles, swaps):
    slots = own_ref.shape[1]
    partner = partner_ref[...]
    own = own_ref[...]
    live = lax.broadcasted_iota(jnp.int32, (1, slots), 1) < count_ref[...]
    outside = partner - n_tiles
    axis = lax.shift_right_logical(outside, 2)
    side = lax.bitwise_and(lax.shift_right_logical(outside, 1), 1)
    within = lax.bitwise_and(outside, 1)
    place = jnp.full_like(partner, -1)
    for k, (ax, phase, _) in enumerate(swaps):
        even = lax.axis_index(AXES[ax]) % 2 == 0
        high = even if phase == 0 else jnp.logical_not(even)
        want = jnp.where(high, 1, 0)
        place = jnp.where((axis == ax) & (side == want), n_tiles + 2 * k + within, place)
    place = jnp.where(outside < 0, partner, place)
    own_hot = jnp.where((row_ids((8, slots)) == own) & live, 1.0, 0.0)
    place_hot = jnp.where(row_ids((32, slots)) == place, 1.0, 0.0)
    return lax.dot_general(own_hot, place_hot, (((1,), (1,)), ((), ())), preferred_element_type=F32)


def slow_totals(u, charge):
    base = jnp.where(row_ids(u.shape) == 3, 1.0, u) * charge
    rows = jnp.concatenate(split3(base), axis=0)
    first = lax.broadcasted_iota(jnp.int32, rows.shape, 1) < LANES
    return jnp.concatenate([jnp.where(first, rows, 0.0), jnp.where(first, 0.0, rows)], axis=0)


def slow_fold(counts, first_tile):
    wide = {}

    def row(it, u):
        if u not in wide:
            wide[u] = jnp.broadcast_to(counts[:, u : u + 1], (8, LANES))
        return jnp.concatenate([wide[u][2 * it : 2 * it + 1], wide[u][2 * it + 1 : 2 * it + 2]], axis=1)

    def fold(it, st, part):
        u = first_tile + 2 * st
        return part[:24] * row(it, u) + part[24:] * row(it, u + 1)

    return fold


def slow_from(u, charge, sums):
    part = sums[0:8] + sums[8:16] + sums[16:24]
    return (LONG_SCALE * LONG_UNIT) * charge * (u * part[3:4] - part)


def slow_own_kernel(swaps, x_ref, charge_ref, own_ref, partner_ref, count_ref, slow_out, counts_out):
    n = x_ref.shape[1]
    charge = charge_ref[...]
    u = scaled(x_ref[...], centre((8, n)), LONG_UNIT)
    pair, _ = source_matrices(u)
    counts = tile_counts(own_ref, partner_ref, count_ref, n // LANES, swaps)
    counts_out[...] = counts
    sums = pair_sums(
        blocks(receiver_matrix(u)),
        [jnp.transpose(p).astype(BF16) for p in blocks(pair)],
        [slow_totals(b, q) for b, q in zip(blocks(u), blocks(charge))],
        slow_fold(counts, 0),
    )
    slow_out[...] = slow_from(u, charge, jnp.concatenate(sums, axis=1))[:3]


def slow_halo_kernel(swaps, *refs):
    x_ref, v_ref, mass_ref, charge_ref, counts_ref, slow_ref, force_ref, start_ref = refs[:8]
    arrived, refs = refs[8 : 8 + len(swaps)], refs[8 + len(swaps) :]
    outs, (moved, v_new, slow_new, sems) = refs[:4], refs[4:]
    x = x_ref[...]
    n = x.shape[1]
    moved[...] = x - start_ref[...]
    copies = [
        pltpu.make_async_copy(src, dst, sems.at[k])
        for k, (src, dst) in enumerate(zip([moved, v_new, force_ref, slow_new], outs))
    ]
    copies[0].start()
    copies[2].start()
    u = scaled(x, centre((8, n)), LONG_UNIT)
    charge = charge_ref[...]
    sources, totals = [], []
    for swap, ref in zip(swaps, arrived):
        got = ref[...]
        there, valid = halo_place(swap, got, LONG_UNIT)
        sources.append(jnp.transpose(source_matrices(there, valid)[0]).astype(BF16))
        totals.append(slow_totals(there, got[3:4]))
    sums = pair_sums(
        blocks(receiver_matrix(u)), sources, totals, slow_fold(counts_ref[...], n // LANES)
    )
    slow = slow_ref[...] + slow_from(u, charge, jnp.concatenate(sums, axis=1))[:3]
    slow_new[...] = slow
    v_new[...] = v_ref[...] + (0.5 * INNER * STEP) * mass_ref[...] * slow
    copies[1].start()
    copies[3].start()
    for c in copies:
        c.wait()


def halo_place(swap, got, unit):
    axis, phase, _ = swap
    place = lax.axis_index(AXES[axis])
    valid = place >= 0
    if phase:
        valid = (place > 0) & (place < lax.axis_size(AXES[axis]) - 1)
    there = scaled(got, centre((8, got.shape[1])), unit)
    return jnp.where(valid, there, 0.0), valid


def own_kernel(first, *refs):
    x_ref, bonds_ref, bond_k_ref = refs[:3]
    out_ref, incidence = refs[3:] if first else (refs[4], refs[3])
    x = x_ref[...]
    n = x.shape[1]
    tiles = lane_tiles(pad8(x))
    pulls = []
    for t in range(n // LANES):
        part = slice(t * LANES, (t + 1) * LANES)
        gap = gather_lanes(tiles, bonds_ref[0:1, part]) - gather_lanes(tiles, bonds_ref[1:2, part])
        pulls.append(bond_k_ref[:, part] * gap)
    pull = jnp.concatenate(pulls, axis=1)
    pull = jnp.concatenate(split3(pull), axis=0).astype(BF16)
    if first:
        for t in range(n // LANES):
            part = slice(t * LANES, (t + 1) * LANES)
            i = jnp.transpose(jnp.broadcast_to(bonds_ref[0:1, part], (LANES, LANES)))
            j = jnp.transpose(jnp.broadcast_to(bonds_ref[1:2, part], (LANES, LANES)))
            for s in range(n // LANES):
                atom = lax.broadcasted_iota(jnp.int32, (LANES, LANES), 1) + s * LANES
                hit = jnp.where(j == atom, 1.0, 0.0)
                hit = jnp.where(i == atom, hit - 1.0, hit)
                incidence[part, s * LANES : (s + 1) * LANES] = hit.astype(BF16)
    bonded = dot(pull, incidence[...])
    bonded = bonded[0:8] + bonded[8:16] + bonded[16:24]

    u = scaled(x, centre((8, n)), SHORT_UNIT)
    pair, total = source_matrices(u)
    sums = pair_sums(
        blocks(receiver_matrix(u)),
        [jnp.transpose(p).astype(BF16) for p in blocks(pair)],
        blocks(total),
    )
    force = short_from(u, jnp.concatenate(sums, axis=1)) + bonded
    out_ref[...] = force[:3]


def halo_kernel(swaps, last, send_charge, *refs):
    x_ref, v_ref, mass_ref, force_ref = refs[:4]
    arrived, refs = refs[4 : 4 + len(swaps)], refs[4 + len(swaps) :]
    x = x_ref[...]
    u = scaled(x, centre((8, x.shape[1])), SHORT_UNIT)
    sources, totals = [], []
    for swap, ref in zip(swaps, arrived):
        pair, total = source_matrices(*halo_place(swap, ref[...], SHORT_UNIT))
        sources.append(jnp.transpose(pair).astype(BF16))
        totals.append(total)
    sums = pair_sums(blocks(receiver_matrix(u)), sources, totals)
    mass = mass_ref[...]
    force = force_ref[...] + short_from(u, jnp.concatenate(sums, axis=1))[:3]
    v = v_ref[...] + (0.5 * STEP) * mass * force
    if last:
        force_out, v_out = refs
        force_out[...] = force
        v_out[...] = v
        return
    index_ref, refs = refs[0], refs[1:]
    charge = None
    if send_charge:
        charge, refs = refs[0][...], refs[1:]
    v = v + (0.5 * STEP) * mass * force
    x = x + STEP * v
    refs[0][...] = x
    refs[1][...] = v
    write_faces(swaps, x, charge, index_ref, refs[2:])


def call(kernel, outs, args, flops=0):
    return pl.pallas_call(
        kernel,
        out_shape=[jax.ShapeDtypeStruct(s, d) for s, d in outs],
        in_specs=[pl.BlockSpec(memory_space=pltpu.VMEM)] * len(args),
        out_specs=[pl.BlockSpec(memory_space=pltpu.VMEM)] * len(outs),
        compiler_params=pltpu.CompilerParams(vmem_limit_bytes=24 * 1024 * 1024),
        cost_estimate=pl.CostEstimate(flops=flops, bytes_accessed=100000, transcendentals=0),
    )(*args)


def on_device(
    swaps,
    positions,
    velocities,
    inv_mass,
    charge,
    fast_force,
    slow_force,
    bonds,
    bond_k,
    halo_index,
    pair_own,
    pair_partner,
    pair_count,
):
    n = positions.shape[1]
    vec = ((3, n), F32)
    sends = [((4, halo_index.shape[1]), F32)] * len(swaps)
    start_args = [positions, inv_mass.reshape(1, n), halo_index, velocities, fast_force, slow_force]
    start_args += [charge.reshape(1, n), bonds, bond_k.reshape(1, -1)]
    start_args += [pair_own.reshape(1, -1), pair_partner.reshape(1, -1), pair_count.reshape(1, 1)]
    assert len(start_args) == N_START
    kept = [(a.shape, a.dtype) for a in start_args[:3] + start_args[6:]]
    start_args = [pltpu.with_memory_space_constraint(a, pltpu.HBM) for a in start_args[:-1]] + start_args[-1:]
    start, mass, index, charge, bonds, bond_k, own, partner, count, x, v, *faces = pl.pallas_call(
        functools.partial(start_kernel, swaps),
        out_shape=[jax.ShapeDtypeStruct(s, d) for s, d in kept + [vec, vec] + sends],
        in_specs=[pl.BlockSpec(memory_space=pltpu.HBM)] * N_START,
        out_specs=[pl.BlockSpec(memory_space=pltpu.VMEM)] * (len(kept) + 2 + len(sends)),
        scratch_shapes=[pltpu.VMEM((3, n), F32)] * 3 + [pltpu.SemaphoreType.DMA((N_START,))],
        compiler_params=pltpu.CompilerParams(vmem_limit_bytes=4 * 1024 * 1024),
    )(*start_args)
    incidence = None
    for turn in range(INNER):
        first, last = turn == 0, turn == INNER - 1
        arrived = [lax.ppermute(f, AXES, perm) for f, (_, _, perm) in zip(faces, swaps)]
        outs, args = [vec], [x, bonds, bond_k]
        if first:
            outs.append(((bonds.shape[1], n), BF16))
        else:
            args.append(incidence)
        force, *built = call(functools.partial(own_kernel, first), outs, args, flops=2 * 10**9)
        if first:
            incidence = built[0]
        args = [x, v, mass, force] + arrived
        if last:
            slow, counts = call(
                functools.partial(slow_own_kernel, swaps),
                [vec, ((8, 32), F32)],
                [x, charge, own, partner, count],
                flops=2 * 10**9,
            )
            force, v = call(
                functools.partial(halo_kernel, swaps, True, False), [vec, vec], args, flops=10**9
            )
            break
        args.append(index)
        send_charge = turn == INNER - 2
        if send_charge:
            args.append(charge)
        x, v, *faces = call(
            functools.partial(halo_kernel, swaps, False, send_charge),
            [vec, vec] + sends,
            args,
            flops=10**9,
        )
    args = [x, v, mass, charge, counts, slow, force, start] + arrived
    return pl.pallas_call(
        functools.partial(slow_halo_kernel, swaps),
        out_shape=[jax.ShapeDtypeStruct(*vec)] * 4,
        in_specs=[pl.BlockSpec(memory_space=pltpu.VMEM)] * len(args),
        out_specs=[pl.BlockSpec(memory_space=pltpu.HBM)] * 4,
        scratch_shapes=[pltpu.VMEM((3, n), F32)] * 3 + [pltpu.SemaphoreType.DMA((4,))],
        compiler_params=pltpu.CompilerParams(vmem_limit_bytes=24 * 1024 * 1024),
    )(*args)


def solution(mesh):
    rows = P(None, AXES)
    flat = P(AXES)
    swaps = matchings([mesh.shape[ax] for ax in AXES])
    return jax.shard_map(
        functools.partial(on_device, swaps),
        mesh=mesh,
        in_specs=(rows, rows, flat, flat, rows, rows, rows, flat, rows, flat, flat, flat),
        out_specs=(rows, rows, rows, rows),
        check_vma=False,
    )
```

time: 51.6 us -> 44.1 us (0.85)
  local copies, waits for them, and re-layouts: 5.66 us -> 0 us
  Pallas kernels: 25.1 us -> 23.4 us
    pallas_call x9, Pallas kernels: 25.1 us -> 19.2 us  [call(): pl.pallas_call(kernel, out_shape=[jax.ShapeDtypeStruct(s, d) for s, d in...]
    unnamed x30 -> x0, local copies, waits for them, and re-layouts: 5.66 us -> none
    pallas_call x0 -> x2, Pallas kernels: none -> 4.15 us  [the longest x1 2.49 us: on_device(): pl.pallas_call(functools.partial(slow_halo_kernel, swaps), out_shape=[jax...]
  transfers between devices with their start and end apart: 20 -> 20, of which waited for: 2 -> 3; matrix products, arithmetic and copies ran while one was open for 0% -> 0% of each run, Pallas kernels for 24% -> 21%
where the time goes in v1:
time: 44.1 us; the launch traced here: 43.9 us
  Pallas kernels  23.4 us (53%)
  starting transfers between devices  17.9 us (41%)
  between operations  1.62 us (4%)
  waiting for transfers between devices  0.99 us (2%)
    pallas_call x9, Pallas kernels, call(): pl.pallas_call(kernel, out_shape=[jax.ShapeDtypeStruct(s, d) for s, d in...  19.2 us
    ppermute x20, starting transfers between devices, on_device(): lax.ppermute(f, AXES, perm)  17.9 us
    pallas_call x1, Pallas kernels, on_device(): pl.pallas_call(functools.partial(slow_halo_kernel, swaps), out_shape=[jax...  2.49 us
    pallas_call x1, Pallas kernels, on_device(): pl.pallas_call(functools.partial(start_kernel, swaps), out_shape=[jax.Sha...  1.66 us
    ppermute x20, waiting for transfers between devices, on_device(): lax.ppermute(f, AXES, perm)  0.99 us
  transfers between devices with their start and end apart: 20, of which 3 were waited for; matrix products, arithmetic and copies ran while one was open for 0% of the time, Pallas kernels for 21%

profile of v1, /device:TPU:0, one launch (start us, length us, event | category | flops | bytes accessed | tf_op | source)
XLA Modules:
  0.0 43.9 jit_solution(5001281457662379883)
XLA Ops:
  1.3 1.7 %shard_map.147 = (f32[3,1024]{1,0:T(4,128)S(1)}, f32[1,1024]{1,0:T(1,128)S(1)}, s32[6,256]{1,0:T(8,128)S(1)}, f32[1,1024]{1,0:T(1,128)S(1)}, s32[2,1024]{1,0:T(2...) custom-call(f32[3,1024]{1,0:T(4,128)} %refs_0_.1, ...), custom_call_target="tpu_custom_call" | custom-call | tf_op jit(solution)/shard_map/pallas_call | solution.py:405
  2.9 3.1 %collective-permute-start = (f32[4,256]{1,0:T(4,128)S(1)}, f32[4,256]{1,0:T(4,128)S(1)}, u32[]{:S(2)}, u32[]{:S(2)}) collective-permute-start(f32[4,256]{1,0:T(4,128)S(1)} %get-tuple-element.53), channel_id=1, source_target_pairs={{0,1},{1,0},{2,3},{3,2},{4,5},{5,4},{6,7},{7,6},{8,9},{9,8},{10,11... | collective-permute-start | bytes 12296 | tf_op jit(solution)/shard_map/ppermute | solution.py:416
  6.1 1.5 %collective-permute-start.2 = (f32[4,256]{1,0:T(4,128)S(1)}, f32[4,256]{1,0:T(4,128)S(1)}, u32[]{:S(2)}, u32[]{:S(2)}) collective-permute-start(f32[4,256]{1,0:T(4,128)S(1)} %get-tuple-element.55), channel_id=1, source_target_pairs={{0,16},{1,17},{2,18},{3,19},{4,20},{5,21},{6,22},{7,23},{8,24},{9,... | collective-permute-start | bytes 12296 | tf_op jit(solution)/shard_map/ppermute | solution.py:416
  7.8 0.5 %collective-permute-start.4 = (f32[4,256]{1,0:T(4,128)S(1)}, f32[4,256]{1,0:T(4,128)S(1)}, u32[]{:S(2)}, u32[]{:S(2)}) collective-permute-start(f32[4,256]{1,0:T(4,128)S(1)} %get-tuple-element.57), channel_id=1, source_target_pairs={{0,16},{1,17},{2,18},{3,19},{4,8},{5,9},{6,10},{7,11},{8,4},{9,5},... | collective-permute-start | bytes 12296 | tf_op jit(solution)/shard_map/ppermute | solution.py:416
  8.3 3.0 %shard_map.148 = (f32[3,1024]{1,0:T(4,128)S(1)}, bf16[1024,1024]{1,0:T(8,128)(2,1)S(1)}) custom-call(f32[3,1024]{1,0:T(4,128)S(1)} %get-tuple-element.47.refs_0_, s32[2,1024]{1,0:T(2,128)S(1)} %get-tuple-element.50.refs_1_, f32[1,1024]{1,0:T(1,128)S(1)} %get-tuple-element.51.refs_2_), custom_call_target="tpu_custom_call" | custom-call | flops 2000000000 | bytes 100000 | tf_op jit(solution)/shard_map/pallas_call | solution.py:371
  11.4 1.9 %shard_map.149 = (f32[3,1024]{1,0:T(4,128)S(1)}, f32[3,1024]{1,0:T(4,128)S(1)}, f32[4,256]{1,0:T(4,128)S(1)}, f32[4,256]{1,0:T(4,128)S(1)}, f32[4,256]{1,0:T(4,1...) custom-call(f32[3,1024]{1,0:T(4,128)S(1)} %get-tuple-element.47.refs_0_, f32[3,1024]{1,0:T(4,128)S(1)} %get-tuple-element.48.refs_1_, ...), custom_call_target="tpu_custom_call" | custom-call | flops 1000000000 | bytes 100000 | tf_op jit(solution)/shard_map/pallas_call | solution.py:371
  13.3 3.0 %collective-permute-start.5 = (f32[4,256]{1,0:T(4,128)S(1)}, f32[4,256]{1,0:T(4,128)S(1)}, u32[]{:S(2)}, u32[]{:S(2)}) collective-permute-start(f32[4,256]{1,0:T(4,128)S(1)} %get-tuple-element.62), channel_id=1, source_target_pairs={{0,1},{1,0},{2,3},{3,2},{4,5},{5,4},{6,7},{7,6},{8,9},{9,8},{10,11... | collective-permute-start | bytes 12296 | tf_op jit(solution)/shard_map/ppermute | solution.py:416
  16.3 0.8 %collective-permute-start.6 = (f32[4,256]{1,0:T(4,128)S(1)}, f32[4,256]{1,0:T(4,128)S(1)}, u32[]{:S(2)}, u32[]{:S(2)}) collective-permute-start(f32[4,256]{1,0:T(4,128)S(1)} %get-tuple-element.63), channel_id=1, source_target_pairs={{0,4},{1,2},{2,1},{3,7},{4,0},{5,6},{6,5},{7,3},{8,12},{9,10},{10,... | collective-permute-start | bytes 12296 | tf_op jit(solution)/shard_map/ppermute | solution.py:416
  17.2 0.7 %collective-permute-start.7 = (f32[4,256]{1,0:T(4,128)S(1)}, f32[4,256]{1,0:T(4,128)S(1)}, u32[]{:S(2)}, u32[]{:S(2)}) collective-permute-start(f32[4,256]{1,0:T(4,128)S(1)} %get-tuple-element.64), channel_id=1, source_target_pairs={{0,16},{1,17},{2,18},{3,19},{4,20},{5,21},{6,22},{7,23},{8,24},{9,... | collective-permute-start | bytes 12296 | tf_op jit(solution)/shard_map/ppermute | solution.py:416
  18.1 1.1 %collective-permute-start.9 = (f32[4,256]{1,0:T(4,128)S(1)}, f32[4,256]{1,0:T(4,128)S(1)}, u32[]{:S(2)}, u32[]{:S(2)}) collective-permute-start(f32[4,256]{1,0:T(4,128)S(1)} %get-tuple-element.66), channel_id=1, source_target_pairs={{0,16},{1,17},{2,18},{3,19},{4,8},{5,9},{6,10},{7,11},{8,4},{9,5},... | collective-permute-start | bytes 12296 | tf_op jit(solution)/shard_map/ppermute | solution.py:416
  19.2 2.1 %shard_map.150.refs_3_ = f32[3,1024]{1,0:T(4,128)S(1)} custom-call(f32[3,1024]{1,0:T(4,128)S(1)} %get-tuple-element.59.refs_0_, s32[2,1024]{1,0:T(2,128)S(1)} %get-tuple-element.50.refs_1_, f32[1,1024]{1,0:T(1,128)S(1)} %get-tuple-element.51.refs_2_, bf16[1024,1024]{1,0:T(8,128)(2,1)S(1)} %get-tuple-element.61.refs_3_), custom_call_target="tpu_custom_call" | custom-call | flops 2000000000 | bytes 100000 | tf_op jit(solution)/shard_map/pallas_call | solution.py:371
  21.7 1.9 %shard_map.151 = (f32[3,1024]{1,0:T(4,128)S(1)}, f32[3,1024]{1,0:T(4,128)S(1)}, f32[4,256]{1,0:T(4,128)S(1)}, f32[4,256]{1,0:T(4,128)S(1)}, f32[4,256]{1,0:T(4,1...) custom-call(f32[3,1024]{1,0:T(4,128)S(1)} %get-tuple-element.59.refs_0_, f32[3,1024]{1,0:T(4,128)S(1)} %get-tuple-element.60.refs_1_, ...), custom_call_target="tpu_custom_call" | custom-call | flops 1000000000 | bytes 100000 | tf_op jit(solution)/shard_map/pallas_call | solution.py:371
  23.6 0.5 %collective-permute-start.10 = (f32[4,256]{1,0:T(4,128)S(1)}, f32[4,256]{1,0:T(4,128)S(1)}, u32[]{:S(2)}, u32[]{:S(2)}) collective-permute-start(f32[4,256]{1,0:T(4,128)S(1)} %get-tuple-element.69), channel_id=1, source_target_pairs={{0,1},{1,0},{2,3},{3,2},{4,5},{5,4},{6,7},{7,6},{8,9},{9,8},{10,11... | collective-permute-start | bytes 12296 | tf_op jit(solution)/shard_map/ppermute | solution.py:416
  24.1 0.9 %collective-permute-start.12 = (f32[4,256]{1,0:T(4,128)S(1)}, f32[4,256]{1,0:T(4,128)S(1)}, u32[]{:S(2)}, u32[]{:S(2)}) collective-permute-start(f32[4,256]{1,0:T(4,128)S(1)} %get-tuple-element.71), channel_id=1, source_target_pairs={{0,16},{1,17},{2,18},{3,19},{4,20},{5,21},{6,22},{7,23},{8,24},{9,... | collective-permute-start | bytes 12296 | tf_op jit(solution)/shard_map/ppermute | solution.py:416
  25.2 1.2 %collective-permute-start.14 = (f32[4,256]{1,0:T(4,128)S(1)}, f32[4,256]{1,0:T(4,128)S(1)}, u32[]{:S(2)}, u32[]{:S(2)}) collective-permute-start(f32[4,256]{1,0:T(4,128)S(1)} %get-tuple-element.73), channel_id=1, source_target_pairs={{0,16},{1,17},{2,18},{3,19},{4,8},{5,9},{6,10},{7,11},{8,4},{9,5},... | collective-permute-start | bytes 12296 | tf_op jit(solution)/shard_map/ppermute | solution.py:416
  26.4 2.1 %shard_map.152.refs_3_ = f32[3,1024]{1,0:T(4,128)S(1)} custom-call(f32[3,1024]{1,0:T(4,128)S(1)} %get-tuple-element.67.refs_0_, s32[2,1024]{1,0:T(2,128)S(1)} %get-tuple-element.50.refs_1_, f32[1,1024]{1,0:T(1,128)S(1)} %get-tuple-element.51.refs_2_, bf16[1024,1024]{1,0:T(8,128)(2,1)S(1)} %get-tuple-element.61.refs_3_), custom_call_target="tpu_custom_call" | custom-call | flops 2000000000 | bytes 100000 | tf_op jit(solution)/shard_map/pallas_call | solution.py:371
  28.8 2.1 %shard_map.153 = (f32[3,1024]{1,0:T(4,128)S(1)}, f32[3,1024]{1,0:T(4,128)S(1)}, f32[4,256]{1,0:T(4,128)S(1)}, f32[4,256]{1,0:T(4,128)S(1)}, f32[4,256]{1,0:T(4,1...) custom-call(f32[3,1024]{1,0:T(4,128)S(1)} %get-tuple-element.67.refs_0_, f32[3,1024]{1,0:T(4,128)S(1)} %get-tuple-element.68.refs_1_, ...), custom_call_target="tpu_custom_call" | custom-call | flops 1000000000 | bytes 100000 | tf_op jit(solution)/shard_map/pallas_call | solution.py:371
  30.9 2.1 %shard_map.154.refs_3_ = f32[3,1024]{1,0:T(4,128)S(1)} custom-call(f32[3,1024]{1,0:T(4,128)S(1)} %get-tuple-element.75.refs_0_.x_ref, s32[2,1024]{1,0:T(2,128)S(1)} %get-tuple-element.50.refs_1_, f32[1,1024]{1,0:T(1,128)S(1)} %get-tuple-element.51.refs_2_, bf16[1024,1024]{1,0:T(8,128)(2,1)S(1)} %get-tuple-element.61.refs_3_), custom_call_target="tpu_custom_call" | custom-call | flops 2000000000 | bytes 100000 | tf_op jit(solution)/shard_map/pallas_call | solution.py:371
  33.0 1.7 %collective-permute-start.15 = (f32[4,256]{1,0:T(4,128)S(1)}, f32[4,256]{1,0:T(4,128)S(1)}, u32[]{:S(2)}, u32[]{:S(2)}) collective-permute-start(f32[4,256]{1,0:T(4,128)S(1)} %get-tuple-element.77), channel_id=1, source_target_pairs={{0,1},{1,0},{2,3},{3,2},{4,5},{5,4},{6,7},{7,6},{8,9},{9,8},{10,11... | collective-permute-start | bytes 12296 | tf_op jit(solution)/shard_map/ppermute | solution.py:416
  34.7 0.9 %collective-permute-start.17 = (f32[4,256]{1,0:T(4,128)S(1)}, f32[4,256]{1,0:T(4,128)S(1)}, u32[]{:S(2)}, u32[]{:S(2)}) collective-permute-start(f32[4,256]{1,0:T(4,128)S(1)} %get-tuple-element.79), channel_id=1, source_target_pairs={{0,16},{1,17},{2,18},{3,19},{4,20},{5,21},{6,22},{7,23},{8,24},{9,... | collective-permute-start | bytes 12296 | tf_op jit(solution)/shard_map/ppermute | solution.py:416
  35.8 1.1 %collective-permute-start.19 = (f32[4,256]{1,0:T(4,128)S(1)}, f32[4,256]{1,0:T(4,128)S(1)}, u32[]{:S(2)}, u32[]{:S(2)}) collective-permute-start(f32[4,256]{1,0:T(4,128)S(1)} %get-tuple-element.81), channel_id=1, source_target_pairs={{0,16},{1,17},{2,18},{3,19},{4,8},{5,9},{6,10},{7,11},{8,4},{9,5},... | collective-permute-start | bytes 12296 | tf_op jit(solution)/shard_map/ppermute | solution.py:416
  36.9 2.1 %shard_map.156 = (f32[3,1024]{1,0:T(4,128)S(1)}, f32[8,32]{1,0:T(8,128)S(1)}) custom-call(f32[3,1024]{1,0:T(4,128)S(1)} %get-tuple-element.75.refs_0_.x_ref, f32[1,1024]{1,0:T(1,128)S(1)} %get-tuple-element.74.refs_10_.charge_ref.refs_3_, s32[1,96]{1,0:T(1,128)S(1)} %get-tuple-element.83.own_ref, s32[1,96]{1,0:T(1,128)S(1)} %get-tuple-element.84.partner_ref, ...), custom_call_target="tpu_custom_call" | custom-call | flops 2000000000 | bytes 100000 | tf_op jit(solution)/shard_map/pallas_call | solution.py:371
  39.4 1.8 %shard_map.155 = (f32[3,1024]{1,0:T(4,128)S(1)}, f32[3,1024]{1,0:T(4,128)S(1)}) custom-call(f32[3,1024]{1,0:T(4,128)S(1)} %get-tuple-element.75.refs_0_.x_ref, f32[3,1024]{1,0:T(4,128)S(1)} %get-tuple-element.76.refs_1_, f32[1,1024]{1,0:T(1,128)S(1)} %get-tuple-element.49.refs_2_, f32[3,1024]{1,0:T(4,128)S(1)} %shard_map.154.refs_3_, ...), custom_call_target="tpu_custom_call" | custom-call | flops 1000000000 | bytes 100000 | tf_op jit(solution)/shard_map/pallas_call | solution.py:371
  41.2 2.5 %shard_map.157 = (f32[3,1024]{1,0:T(4,128)}, f32[3,1024]{1,0:T(4,128)}, f32[3,1024]{1,0:T(4,128)}, f32[3,1024]{1,0:T(4,128)}) custom-call(f32[3,1024]{1,0:T(4,128)S(1)} %get-tuple-element.75.refs_0_.x_ref, f32[3,1024]{1,0:T(4,128)S(1)} %get-tuple-element.82.refs_1_, f32[1,1024]{1,0:T(1,128)S(1)} %get-tuple-element.49.refs_2_, ...), custom_call_target="tpu_custom_call" | custom-call | tf_op jit(solution)/shard_map/pallas_call | solution.py:448
  (27 shorter events, 1.9 us)
Async XLA Ops:
  2.9 8.4 %collective-permute-start = (f32[4,256]{1,0:T(4,128)S(1)}, f32[4,256]{1,0:T(4,128)S(1)}, u32[]{:S(2)}, u32[]{:S(2)}) collective-permute-start(f32[4,256]{1,0:T(4,128)S(1)} %get-tuple-element.53), channel_id=1, source_target_pairs={{0,1},{1,0},{2,3},{3,2},{4,5},{5,4},{6,7},{7,6},{8,9},{9,8},{10,11... | collective-permute-start | bytes 12296 | tf_op jit(solution)/shard_map/ppermute | solution.py:416
  6.1 5.3 %collective-permute-start.1 = (f32[4,256]{1,0:T(4,128)S(1)}, f32[4,256]{1,0:T(4,128)S(1)}, u32[]{:S(2)}, u32[]{:S(2)}) collective-permute-start(f32[4,256]{1,0:T(4,128)S(1)} %get-tuple-element.54), channel_id=1, source_target_pairs={{0,4},{1,2},{2,1},{3,7},{4,0},{5,6},{6,5},{7,3},{8,12},{9,10},{10,... | collective-permute-start | bytes 12296 | tf_op jit(solution)/shard_map/ppermute | solution.py:416
  6.1 5.3 %collective-permute-start.2 = (f32[4,256]{1,0:T(4,128)S(1)}, f32[4,256]{1,0:T(4,128)S(1)}, u32[]{:S(2)}, u32[]{:S(2)}) collective-permute-start(f32[4,256]{1,0:T(4,128)S(1)} %get-tuple-element.55), channel_id=1, source_target_pairs={{0,16},{1,17},{2,18},{3,19},{4,20},{5,21},{6,22},{7,23},{8,24},{9,... | collective-permute-start | bytes 12296 | tf_op jit(solution)/shard_map/ppermute | solution.py:416
  7.6 3.8 %collective-permute-start.3 = (f32[4,256]{1,0:T(4,128)S(1)}, f32[4,256]{1,0:T(4,128)S(1)}, u32[]{:S(2)}, u32[]{:S(2)}) collective-permute-start(f32[4,256]{1,0:T(4,128)S(1)} %get-tuple-element.56), channel_id=1, source_target_pairs={{0,4},{1,5},{2,6},{3,7},{4,0},{5,1},{6,2},{7,3},{8,12},{9,13},{10,... | collective-permute-start | bytes 12296 | tf_op jit(solution)/shard_map/ppermute | solution.py:416
  7.8 3.6 %collective-permute-start.4 = (f32[4,256]{1,0:T(4,128)S(1)}, f32[4,256]{1,0:T(4,128)S(1)}, u32[]{:S(2)}, u32[]{:S(2)}) collective-permute-start(f32[4,256]{1,0:T(4,128)S(1)} %get-tuple-element.57), channel_id=1, source_target_pairs={{0,16},{1,17},{2,18},{3,19},{4,8},{5,9},{6,10},{7,11},{8,4},{9,5},... | collective-permute-start | bytes 12296 | tf_op jit(solution)/shard_map/ppermute | solution.py:416
  13.3 8.0 %collective-permute-start.5 = (f32[4,256]{1,0:T(4,128)S(1)}, f32[4,256]{1,0:T(4,128)S(1)}, u32[]{:S(2)}, u32[]{:S(2)}) collective-permute-start(f32[4,256]{1,0:T(4,128)S(1)} %get-tuple-element.62), channel_id=1, source_target_pairs={{0,1},{1,0},{2,3},{3,2},{4,5},{5,4},{6,7},{7,6},{8,9},{9,8},{10,11... | collective-permute-start | bytes 12296 | tf_op jit(solution)/shard_map/ppermute | solution.py:416
  16.3 5.0 %collective-permute-start.6 = (f32[4,256]{1,0:T(4,128)S(1)}, f32[4,256]{1,0:T(4,128)S(1)}, u32[]{:S(2)}, u32[]{:S(2)}) collective-permute-start(f32[4,256]{1,0:T(4,128)S(1)} %get-tuple-element.63), channel_id=1, source_target_pairs={{0,4},{1,2},{2,1},{3,7},{4,0},{5,6},{6,5},{7,3},{8,12},{9,10},{10,... | collective-permute-start | bytes 12296 | tf_op jit(solution)/shard_map/ppermute | solution.py:416
  17.2 4.2 %collective-permute-start.7 = (f32[4,256]{1,0:T(4,128)S(1)}, f32[4,256]{1,0:T(4,128)S(1)}, u32[]{:S(2)}, u32[]{:S(2)}) collective-permute-start(f32[4,256]{1,0:T(4,128)S(1)} %get-tuple-element.64), channel_id=1, source_target_pairs={{0,16},{1,17},{2,18},{3,19},{4,20},{5,21},{6,22},{7,23},{8,24},{9,... | collective-permute-start | bytes 12296 | tf_op jit(solution)/shard_map/ppermute | solution.py:416
  17.8 3.5 %collective-permute-start.8 = (f32[4,256]{1,0:T(4,128)S(1)}, f32[4,256]{1,0:T(4,128)S(1)}, u32[]{:S(2)}, u32[]{:S(2)}) collective-permute-start(f32[4,256]{1,0:T(4,128)S(1)} %get-tuple-element.65), channel_id=1, source_target_pairs={{0,4},{1,5},{2,6},{3,7},{4,0},{5,1},{6,2},{7,3},{8,12},{9,13},{10,... | collective-permute-start | bytes 12296 | tf_op jit(solution)/shard_map/ppermute | solution.py:416
  18.1 3.6 %collective-permute-start.9 = (f32[4,256]{1,0:T(4,128)S(1)}, f32[4,256]{1,0:T(4,128)S(1)}, u32[]{:S(2)}, u32[]{:S(2)}) collective-permute-start(f32[4,256]{1,0:T(4,128)S(1)} %get-tuple-element.66), channel_id=1, source_target_pairs={{0,16},{1,17},{2,18},{3,19},{4,8},{5,9},{6,10},{7,11},{8,4},{9,5},... | collective-permute-start | bytes 12296 | tf_op jit(solution)/shard_map/ppermute | solution.py:416
  23.6 4.9 %collective-permute-start.10 = (f32[4,256]{1,0:T(4,128)S(1)}, f32[4,256]{1,0:T(4,128)S(1)}, u32[]{:S(2)}, u32[]{:S(2)}) collective-permute-start(f32[4,256]{1,0:T(4,128)S(1)} %get-tuple-element.69), channel_id=1, source_target_pairs={{0,1},{1,0},{2,3},{3,2},{4,5},{5,4},{6,7},{7,6},{8,9},{9,8},{10,11... | collective-permute-start | bytes 12296 | tf_op jit(solution)/shard_map/ppermute | solution.py:416
  24.1 4.4 %collective-permute-start.11 = (f32[4,256]{1,0:T(4,128)S(1)}, f32[4,256]{1,0:T(4,128)S(1)}, u32[]{:S(2)}, u32[]{:S(2)}) collective-permute-start(f32[4,256]{1,0:T(4,128)S(1)} %get-tuple-element.70), channel_id=1, source_target_pairs={{0,4},{1,2},{2,1},{3,7},{4,0},{5,6},{6,5},{7,3},{8,12},{9,10},{10,... | collective-permute-start | bytes 12296 | tf_op jit(solution)/shard_map/ppermute | solution.py:416
  24.1 4.4 %collective-permute-start.12 = (f32[4,256]{1,0:T(4,128)S(1)}, f32[4,256]{1,0:T(4,128)S(1)}, u32[]{:S(2)}, u32[]{:S(2)}) collective-permute-start(f32[4,256]{1,0:T(4,128)S(1)} %get-tuple-element.71), channel_id=1, source_target_pairs={{0,16},{1,17},{2,18},{3,19},{4,20},{5,21},{6,22},{7,23},{8,24},{9,... | collective-permute-start | bytes 12296 | tf_op jit(solution)/shard_map/ppermute | solution.py:416
  25.0 3.5 %collective-permute-start.13 = (f32[4,256]{1,0:T(4,128)S(1)}, f32[4,256]{1,0:T(4,128)S(1)}, u32[]{:S(2)}, u32[]{:S(2)}) collective-permute-start(f32[4,256]{1,0:T(4,128)S(1)} %get-tuple-element.72), channel_id=1, source_target_pairs={{0,4},{1,5},{2,6},{3,7},{4,0},{5,1},{6,2},{7,3},{8,12},{9,13},{10,... | collective-permute-start | bytes 12296 | tf_op jit(solution)/shard_map/ppermute | solution.py:416
  25.2 3.6 %collective-permute-start.14 = (f32[4,256]{1,0:T(4,128)S(1)}, f32[4,256]{1,0:T(4,128)S(1)}, u32[]{:S(2)}, u32[]{:S(2)}) collective-permute-start(f32[4,256]{1,0:T(4,128)S(1)} %get-tuple-element.73), channel_id=1, source_target_pairs={{0,16},{1,17},{2,18},{3,19},{4,8},{5,9},{6,10},{7,11},{8,4},{9,5},... | collective-permute-start | bytes 12296 | tf_op jit(solution)/shard_map/ppermute | solution.py:416
  33.0 6.1 %collective-permute-start.15 = (f32[4,256]{1,0:T(4,128)S(1)}, f32[4,256]{1,0:T(4,128)S(1)}, u32[]{:S(2)}, u32[]{:S(2)}) collective-permute-start(f32[4,256]{1,0:T(4,128)S(1)} %get-tuple-element.77), channel_id=1, source_target_pairs={{0,1},{1,0},{2,3},{3,2},{4,5},{5,4},{6,7},{7,6},{8,9},{9,8},{10,11... | collective-permute-start | bytes 12296 | tf_op jit(solution)/shard_map/ppermute | solution.py:416
  34.7 4.4 %collective-permute-start.16 = (f32[4,256]{1,0:T(4,128)S(1)}, f32[4,256]{1,0:T(4,128)S(1)}, u32[]{:S(2)}, u32[]{:S(2)}) collective-permute-start(f32[4,256]{1,0:T(4,128)S(1)} %get-tuple-element.78), channel_id=1, source_target_pairs={{0,4},{1,2},{2,1},{3,7},{4,0},{5,6},{6,5},{7,3},{8,12},{9,10},{10,... | collective-permute-start | bytes 12296 | tf_op jit(solution)/shard_map/ppermute | solution.py:416
  34.7 4.4 %collective-permute-start.17 = (f32[4,256]{1,0:T(4,128)S(1)}, f32[4,256]{1,0:T(4,128)S(1)}, u32[]{:S(2)}, u32[]{:S(2)}) collective-permute-start(f32[4,256]{1,0:T(4,128)S(1)} %get-tuple-element.79), channel_id=1, source_target_pairs={{0,16},{1,17},{2,18},{3,19},{4,20},{5,21},{6,22},{7,23},{8,24},{9,... | collective-permute-start | bytes 12296 | tf_op jit(solution)/shard_map/ppermute | solution.py:416
  35.6 3.5 %collective-permute-start.18 = (f32[4,256]{1,0:T(4,128)S(1)}, f32[4,256]{1,0:T(4,128)S(1)}, u32[]{:S(2)}, u32[]{:S(2)}) collective-permute-start(f32[4,256]{1,0:T(4,128)S(1)} %get-tuple-element.80), channel_id=1, source_target_pairs={{0,4},{1,5},{2,6},{3,7},{4,0},{5,1},{6,2},{7,3},{8,12},{9,13},{10,... | collective-permute-start | bytes 12296 | tf_op jit(solution)/shard_map/ppermute | solution.py:416
  35.8 3.6 %collective-permute-start.19 = (f32[4,256]{1,0:T(4,128)S(1)}, f32[4,256]{1,0:T(4,128)S(1)}, u32[]{:S(2)}, u32[]{:S(2)}) collective-permute-start(f32[4,256]{1,0:T(4,128)S(1)} %get-tuple-element.81), channel_id=1, source_target_pairs={{0,16},{1,17},{2,18},{3,19},{4,8},{5,9},{6,10},{7,11},{8,4},{9,5},... | collective-permute-start | bytes 12296 | tf_op jit(solution)/shard_map/ppermute | solution.py:416

commit v2 on v1

--- a/solution.py
+++ b/solution.py
@@ -27,24 +27,25 @@
     nx, ny, nz = sizes
     assert nx % 2 == 0 and ny % 2 == 0 and nz % 2 == 0
     swaps = []
-    for axis in (2, 0, 1):
-        for phase in range(1 if sizes[axis] == 2 else 2):
-            perm = []
-            for a in range(nx):
-                for b in range(ny):
-                    for c in range(nz):
-                        place = [a, b, c]
-                        p = place[axis]
-                        partner = p ^ 1 if phase == 0 else (p + 1 if p % 2 else p - 1)
-                        if 0 <= partner < sizes[axis]:
-                            place[axis] = partner
-                        else:
-                            other = 0 if axis == 1 else 1
-                            place[other] ^= 1
-                        perm.append(
-                            ((a * ny + b) * nz + c, (place[0] * ny + place[1]) * nz + place[2])
-                        )
-            swaps.append((axis, phase, perm))
+    for axis, phase in ((2, 0), (2, 1), (1, 1), (0, 0), (0, 1), (1, 0)):
+        if phase and sizes[axis] == 2:
+            continue
+        perm = []
+        for a in range(nx):
+            for b in range(ny):
+                for c in range(nz):
+                    place = [a, b, c]
+                    p = place[axis]
+                    partner = p ^ 1 if phase == 0 else (p + 1 if p % 2 else p - 1)
+                    if 0 <= partner < sizes[axis]:
+                        place[axis] = partner
+                    elif axis == 1:
+                        place[1] = ny - 1 - p
+                    else:
+                        place[1] ^= 1
+                    source = (a * ny + b) * nz + c
+                    perm.append((source, (place[0] * ny + place[1]) * nz + place[2]))
+        swaps.append((axis, phase, perm))
     return swaps
 
 
@@ -114,43 +115,61 @@
     return w, w - rounded(w)
 
 
-def gather_lanes(sources, index):
-    index = jnp.broadcast_to(index, (8, LANES))
+def pad8(x):
+    return jnp.concatenate([x, jnp.zeros((8 - x.shape[0], x.shape[1]), F32)], axis=0)
+
+
+def gather_grid(x, index):
     tile = lax.shift_right_logical(index, 7)
     lane = lax.bitwise_and(index, LANES - 1)
-    out = jnp.zeros((8, LANES), F32)
-    for r, src in enumerate(sources):
-        out = jnp.where(tile == r, jnp.take_along_axis(src, lane, axis=1), out)
+    hits = [tile == r for r in range(1, x.shape[1] // LANES)]
+    out = []
+    for c in range(x.shape[0]):
+        got = None
+        for r in range(x.shape[1] // LANES):
+            row = jnp.broadcast_to(x[c : c + 1, r * LANES : (r + 1) * LANES], (8, LANES))
+            here = jnp.take_along_axis(row, lane, axis=1)
+            got = here if got is None else jnp.where(hits[r - 1], here, got)
+        out.append(got)
     return out
 
 
-def lane_tiles(a):
-    return [a[:, r * LANES : (r + 1) * LANES] for r in range(a.shape[1] // LANES)]
-
-
-def pad8(x):
-    return jnp.concatenate([x, jnp.zeros((8 - x.shape[0], x.shape[1]), F32)], axis=0)
-
-
-def write_faces(swaps, x, charge, index_ref, send_refs):
-    rows = [x] if charge is None else [x, charge]
-    tiles = lane_tiles(pad8(jnp.concatenate(rows, axis=0)))
-    for (axis, phase, _), ref in zip(swaps, send_refs):
+def write_faces(x, index_ref, send_refs):
+    per = send_refs[0].shape[1] // LANES
+    for g in range(index_ref.shape[0] // 8):
+        got = gather_grid(x, index_ref[8 * g : 8 * g + 8, :])
+        for r in range(8 * g, min(8 * g + 8, per * len(send_refs))):
+            part = slice(r % per * LANES, (r % per + 1) * LANES)
+            for c, rows in enumerate(got):
+                send_refs[r // per][c : c + 1, part] = rows[r % 8 : r % 8 + 1]
+
+
+def write_face_index(swaps, index_ref, out_ref):
+    per = index_ref.shape[1] // LANES
+    out_ref[...] = jnp.zeros_like(out_ref)
+    for k, (axis, phase, _) in enumerate(swaps):
         even = lax.axis_index(AXES[axis]) % 2 == 0
         high = even if phase == 0 else jnp.logical_not(even)
-        index = jnp.where(high, index_ref[2 * axis + 1 : 2 * axis + 2, :], index_ref[2 * axis : 2 * axis + 1, :])
-        for w in range(index.shape[1] // LANES):
-            part = slice(w * LANES, (w + 1) * LANES)
-            ref[:, part] = gather_lanes(tiles, index[:, part])[:4]
+        low_row, high_row = index_ref[2 * axis : 2 * axis + 1, :], index_ref[2 * axis + 1 : 2 * axis + 2, :]
+        row = jnp.where(high, high_row, low_row)
+        for w in range(per):
+            out_ref[per * k + w : per * k + w + 1, :] = row[:, w * LANES : (w + 1) * LANES]
+
+
+def write_grid(row_ref, out_ref):
+    for t in range(out_ref.shape[1]):
+        for e in range(out_ref.shape[0]):
+            out_ref[e, t : t + 1, :] = row_ref[e : e + 1, t * LANES : (t + 1) * LANES]
 
 
 def start_kernel(swaps, *refs):
     sources, refs = refs[:N_START], refs[N_START:]
-    x_ref, mass_ref, index_ref = refs[:3]
-    kept, refs = refs[3 : N_START - 3], refs[N_START - 3 :]
-    x_out, v_out = refs[:2]
-    send_refs, (v_ref, fast_ref, slow_ref, sems) = refs[2 : 2 + len(swaps)], refs[2 + len(swaps) :]
-    kept = [x_ref, mass_ref, index_ref, v_ref, fast_ref, slow_ref, *kept]
+    x_ref, mass_ref, charge_ref, own_ref, partner_ref, count_ref = refs[:6]
+    index_out, bonds_out, bond_k_out, x_out, v_out = refs[6:11]
+    send_refs, refs = refs[11 : 11 + len(swaps)], refs[11 + len(swaps) :]
+    v_ref, fast_ref, slow_ref, index_ref, bonds_ref, bond_k_ref, sems = refs
+    kept = [x_ref, mass_ref, index_ref, v_ref, fast_ref, slow_ref]
+    kept += [charge_ref, bonds_ref, bond_k_ref, own_ref, partner_ref, count_ref]
     copies = [
         pltpu.make_async_copy(src, dst, sems.at[k]) for k, (src, dst) in enumerate(zip(sources, kept))
     ]
@@ -158,15 +177,18 @@
         c.start()
     for c in copies[:6]:
         c.wait()
+    write_face_index(swaps, index_ref, index_out)
     mass = mass_ref[...]
     v = v_ref[...] + (0.5 * INNER * STEP) * mass * slow_ref[...]
     v = v + (0.5 * STEP) * mass * fast_ref[...]
     x = x_ref[...] + STEP * v
     x_out[...] = x
     v_out[...] = v
-    write_faces(swaps, x, None, index_ref, send_refs)
+    write_faces(x, index_out, send_refs)
     for c in copies[6:]:
         c.wait()
+    write_grid(bonds_ref, bonds_out)
+    write_grid(bond_k_ref, bond_k_out)
 
 
 def pair_sums(receivers, sources, totals, fold=None):
@@ -305,19 +327,20 @@
     out_ref, incidence = refs[3:] if first else (refs[4], refs[3])
     x = x_ref[...]
     n = x.shape[1]
-    tiles = lane_tiles(pad8(x))
     pulls = []
-    for t in range(n // LANES):
-        part = slice(t * LANES, (t + 1) * LANES)
-        gap = gather_lanes(tiles, bonds_ref[0:1, part]) - gather_lanes(tiles, bonds_ref[1:2, part])
-        pulls.append(bond_k_ref[:, part] * gap)
-    pull = jnp.concatenate(pulls, axis=1)
+    for g in range(bonds_ref.shape[1] // 8):
+        rows = slice(8 * g, 8 * g + 8)
+        ends = zip(gather_grid(x, bonds_ref[0, rows, :]), gather_grid(x, bonds_ref[1, rows, :]))
+        pull = [bond_k_ref[0, rows, :] * (i - j) for i, j in ends]
+        for t in range(8):
+            pulls.append(jnp.concatenate([p[t : t + 1] for p in pull], axis=0))
+    pull = pad8(jnp.concatenate(pulls, axis=1))
     pull = jnp.concatenate(split3(pull), axis=0).astype(BF16)
     if first:
-        for t in range(n // LANES):
+        for t in range(bonds_ref.shape[1]):
             part = slice(t * LANES, (t + 1) * LANES)
-            i = jnp.transpose(jnp.broadcast_to(bonds_ref[0:1, part], (LANES, LANES)))
-            j = jnp.transpose(jnp.broadcast_to(bonds_ref[1:2, part], (LANES, LANES)))
+            i = jnp.transpose(jnp.broadcast_to(bonds_ref[0, t : t + 1, :], (LANES, LANES)))
+            j = jnp.transpose(jnp.broadcast_to(bonds_ref[1, t : t + 1, :], (LANES, LANES)))
             for s in range(n // LANES):
                 atom = lax.broadcasted_iota(jnp.int32, (LANES, LANES), 1) + s * LANES
                 hit = jnp.where(j == atom, 1.0, 0.0)
@@ -364,7 +387,9 @@
     x = x + STEP * v
     refs[0][...] = x
     refs[1][...] = v
-    write_faces(swaps, x, charge, index_ref, refs[2:])
+    if send_charge:
+        x = jnp.concatenate([x, charge], axis=0)
+    write_faces(x, index_ref, refs[2:])
 
 
 def call(kernel, outs, args, flops=0):
@@ -400,14 +425,22 @@
     start_args += [charge.reshape(1, n), bonds, bond_k.reshape(1, -1)]
     start_args += [pair_own.reshape(1, -1), pair_partner.reshape(1, -1), pair_count.reshape(1, 1)]
     assert len(start_args) == N_START
-    kept = [(a.shape, a.dtype) for a in start_args[:3] + start_args[6:]]
+    kept = [(start_args[k].shape, start_args[k].dtype) for k in (0, 1, 6, 9, 10, 11)]
+    n_bonds = bonds.shape[1]
+    face_rows = len(swaps) * halo_index.shape[1] // LANES
+    kept.append(((-(-face_rows // 8) * 8, LANES), jnp.int32))
+    kept.append(((2, n_bonds // LANES, LANES), jnp.int32))
+    kept.append(((1, n_bonds // LANES, LANES), F32))
+    scratch = [pltpu.VMEM((3, n), F32)] * 3
+    scratch += [pltpu.VMEM(halo_index.shape, jnp.int32), pltpu.VMEM(bonds.shape, jnp.int32)]
+    scratch += [pltpu.VMEM((1, n_bonds), F32), pltpu.SemaphoreType.DMA((N_START,))]
     start_args = [pltpu.with_memory_space_constraint(a, pltpu.HBM) for a in start_args[:-1]] + start_args[-1:]
-    start, mass, index, charge, bonds, bond_k, own, partner, count, x, v, *faces = pl.pallas_call(
+    start, mass, charge, own, partner, count, index, bonds, bond_k, x, v, *faces = pl.pallas_call(
         functools.partial(start_kernel, swaps),
         out_shape=[jax.ShapeDtypeStruct(s, d) for s, d in kept + [vec, vec] + sends],
         in_specs=[pl.BlockSpec(memory_space=pltpu.HBM)] * N_START,
         out_specs=[pl.BlockSpec(memory_space=pltpu.VMEM)] * (len(kept) + 2 + len(sends)),
-        scratch_shapes=[pltpu.VMEM((3, n), F32)] * 3 + [pltpu.SemaphoreType.DMA((N_START,))],
+        scratch_shapes=scratch,
         compiler_params=pltpu.CompilerParams(vmem_limit_bytes=4 * 1024 * 1024),
     )(*start_args)
     incidence = None
@@ -416,7 +449,7 @@
         arrived = [lax.ppermute(f, AXES, perm) for f, (_, _, perm) in zip(faces, swaps)]
         outs, args = [vec], [x, bonds, bond_k]
         if first:
-            outs.append(((bonds.shape[1], n), BF16))
+            outs.append(((n_bonds, n), BF16))
         else:
             args.append(incidence)
         force, *built = call(functools.partial(own_kernel, first), outs, args, flops=2 * 10**9)

time: 44.1 us -> 42.8 us (0.971)
  starting transfers between devices: 17.9 us -> 15.6 us
  waiting for transfers between devices: 0.99 us -> 2.74 us
  Pallas kernels: 23.4 us -> 22.6 us
    ppermute x20, starting transfers between devices: 17.9 us -> 15.6 us  [on_device(): lax.ppermute(f, AXES, perm)]
    ppermute x20, waiting for transfers between devices: 0.99 us -> 2.74 us  [on_device(): lax.ppermute(f, AXES, perm)]
    pallas_call x9, Pallas kernels: 19.2 us -> 18.5 us  [call(): pl.pallas_call(kernel, out_shape=[jax.ShapeDtypeStruct(s, d) for s, d in...]
where the time goes in v2:
time: 42.8 us; the launch traced here: 42.5 us
  Pallas kernels  22.6 us (53%)
  starting transfers between devices  15.6 us (36%)
  waiting for transfers between devices  2.74 us (6%)
  between operations  1.61 us (4%)
    pallas_call x9, Pallas kernels, call(): pl.pallas_call(kernel, out_shape=[jax.ShapeDtypeStruct(s, d) for s, d in...  18.5 us
    ppermute x20, starting transfers between devices, on_device(): lax.ppermute(f, AXES, perm)  15.6 us
    ppermute x20, waiting for transfers between devices, on_device(): lax.ppermute(f, AXES, perm)  2.74 us
    pallas_call x1, Pallas kernels, on_device(): pl.pallas_call(functools.partial(slow_halo_kernel, swaps), out_shape=[jax...  2.48 us
    pallas_call x1, Pallas kernels, on_device(): pl.pallas_call(functools.partial(start_kernel, swaps), out_shape=[jax.Sha...  1.61 us
  transfers between devices with their start and end apart: 20, of which 3 were waited for; matrix products, arithmetic and copies ran while one was open for 0% of the time, Pallas kernels for 21%

profile of v2, /device:TPU:0, one launch (start us, length us, event | category | flops | bytes accessed | tf_op | source)
XLA Modules:
  0.0 42.5 jit_solution(15498150688343654853)
XLA Ops:
  1.3 1.6 %shard_map.147 = (f32[3,1024]{1,0:T(4,128)S(1)}, f32[1,1024]{1,0:T(1,128)S(1)}, f32[1,1024]{1,0:T(1,128)S(1)}, s32[1,96]{1,0:T(1,128)S(1)}, s32[1,96]{1,0:T(1,12...) custom-call(f32[3,1024]{1,0:T(4,128)} %refs_0_.1, ...), custom_call_target="tpu_custom_call" | custom-call | tf_op jit(solution)/shard_map/pallas_call | solution.py:438
  2.9 3.1 %collective-permute-start = (f32[4,256]{1,0:T(4,128)S(1)}, f32[4,256]{1,0:T(4,128)S(1)}, u32[]{:S(2)}, u32[]{:S(2)}) collective-permute-start(f32[4,256]{1,0:T(4,128)S(1)} %get-tuple-element.53), channel_id=1, source_target_pairs={{0,1},{1,0},{2,3},{3,2},{4,5},{5,4},{6,7},{7,6},{8,9},{9,8},{10,11... | collective-permute-start | bytes 12296 | tf_op jit(solution)/shard_map/ppermute | solution.py:449
  6.0 1.6 %collective-permute-start.2 = (f32[4,256]{1,0:T(4,128)S(1)}, f32[4,256]{1,0:T(4,128)S(1)}, u32[]{:S(2)}, u32[]{:S(2)}) collective-permute-start(f32[4,256]{1,0:T(4,128)S(1)} %get-tuple-element.55), channel_id=1, source_target_pairs={{0,12},{1,13},{2,14},{3,15},{4,8},{5,9},{6,10},{7,11},{8,4},{9,5},... | collective-permute-start | bytes 12296 | tf_op jit(solution)/shard_map/ppermute | solution.py:449
  7.6 1.5 %collective-permute-start.3 = (f32[4,256]{1,0:T(4,128)S(1)}, f32[4,256]{1,0:T(4,128)S(1)}, u32[]{:S(2)}, u32[]{:S(2)}) collective-permute-start(f32[4,256]{1,0:T(4,128)S(1)} %get-tuple-element.56), channel_id=1, source_target_pairs={{0,16},{1,17},{2,18},{3,19},{4,20},{5,21},{6,22},{7,23},{8,24},{9,... | collective-permute-start | bytes 12296 | tf_op jit(solution)/shard_map/ppermute | solution.py:449
  9.1 2.8 %shard_map.148 = (f32[3,1024]{1,0:T(4,128)S(1)}, bf16[1024,1024]{1,0:T(8,128)(2,1)S(1)}) custom-call(f32[3,1024]{1,0:T(4,128)S(1)} %get-tuple-element.47.refs_0_, s32[2,8,128]{2,1,0:T(8,128)S(1)} %get-tuple-element.50.refs_1_, f32[1,8,128]{2,1,0:T(8,128)S(1)} %get-tuple-element.51.refs_2_), custom_call_target="tpu_custom_call" | custom-call | flops 2000000000 | bytes 100000 | tf_op jit(solution)/shard_map/pallas_call | solution.py:396
  12.1 1.9 %shard_map.149 = (f32[3,1024]{1,0:T(4,128)S(1)}, f32[3,1024]{1,0:T(4,128)S(1)}, f32[4,256]{1,0:T(4,128)S(1)}, f32[4,256]{1,0:T(4,128)S(1)}, f32[4,256]{1,0:T(4,1...) custom-call(f32[3,1024]{1,0:T(4,128)S(1)} %get-tuple-element.47.refs_0_, f32[3,1024]{1,0:T(4,128)S(1)} %get-tuple-element.48.refs_1_, ...), custom_call_target="tpu_custom_call" | custom-call | flops 1000000000 | bytes 100000 | tf_op jit(solution)/shard_map/pallas_call | solution.py:396
  14.0 2.9 %collective-permute-start.5 = (f32[4,256]{1,0:T(4,128)S(1)}, f32[4,256]{1,0:T(4,128)S(1)}, u32[]{:S(2)}, u32[]{:S(2)}) collective-permute-start(f32[4,256]{1,0:T(4,128)S(1)} %get-tuple-element.62), channel_id=1, source_target_pairs={{0,1},{1,0},{2,3},{3,2},{4,5},{5,4},{6,7},{7,6},{8,9},{9,8},{10,11... | collective-permute-start | bytes 12296 | tf_op jit(solution)/shard_map/ppermute | solution.py:449
  16.9 0.6 %collective-permute-start.7 = (f32[4,256]{1,0:T(4,128)S(1)}, f32[4,256]{1,0:T(4,128)S(1)}, u32[]{:S(2)}, u32[]{:S(2)}) collective-permute-start(f32[4,256]{1,0:T(4,128)S(1)} %get-tuple-element.64), channel_id=1, source_target_pairs={{0,12},{1,13},{2,14},{3,15},{4,8},{5,9},{6,10},{7,11},{8,4},{9,5},... | collective-permute-start | bytes 12296 | tf_op jit(solution)/shard_map/ppermute | solution.py:449
  18.1 1.9 %shard_map.150.refs_3_ = f32[3,1024]{1,0:T(4,128)S(1)} custom-call(f32[3,1024]{1,0:T(4,128)S(1)} %get-tuple-element.59.refs_0_, s32[2,8,128]{2,1,0:T(8,128)S(1)} %get-tuple-element.50.refs_1_, f32[1,8,128]{2,1,0:T(8,128)S(1)} %get-tuple-element.51.refs_2_, bf16[1024,1024]{1,0:T(8,128)(2,1)S(1)} %get-tuple-element.61.refs_3_), custom_call_target="tpu_custom_call" | custom-call | flops 2000000000 | bytes 100000 | tf_op jit(solution)/shard_map/pallas_call | solution.py:396
  20.0 1.1 %collective-permute-done.8.refs_7_ = f32[4,256]{1,0:T(4,128)S(1)} collective-permute-done((f32[4,256]{1,0:T(4,128)S(1)}, f32[4,256]{1,0:T(4,128)S(1)}, u32[]{:S(2)}, u32[]{:S(2)}) %collective-permute-start.8) | collective-permute-done | bytes 4128 | tf_op jit(solution)/shard_map/ppermute | solution.py:449
  21.1 1.9 %shard_map.151 = (f32[3,1024]{1,0:T(4,128)S(1)}, f32[3,1024]{1,0:T(4,128)S(1)}, f32[4,256]{1,0:T(4,128)S(1)}, f32[4,256]{1,0:T(4,128)S(1)}, f32[4,256]{1,0:T(4,1...) custom-call(f32[3,1024]{1,0:T(4,128)S(1)} %get-tuple-element.59.refs_0_, f32[3,1024]{1,0:T(4,128)S(1)} %get-tuple-element.60.refs_1_, ...), custom_call_target="tpu_custom_call" | custom-call | flops 1000000000 | bytes 100000 | tf_op jit(solution)/shard_map/pallas_call | solution.py:396
  23.3 1.6 %collective-permute-start.12 = (f32[4,256]{1,0:T(4,128)S(1)}, f32[4,256]{1,0:T(4,128)S(1)}, u32[]{:S(2)}, u32[]{:S(2)}) collective-permute-start(f32[4,256]{1,0:T(4,128)S(1)} %get-tuple-element.71), channel_id=1, source_target_pairs={{0,12},{1,13},{2,14},{3,15},{4,8},{5,9},{6,10},{7,11},{8,4},{9,5},... | collective-permute-start | bytes 12296 | tf_op jit(solution)/shard_map/ppermute | solution.py:449
  24.9 0.7 %collective-permute-start.13 = (f32[4,256]{1,0:T(4,128)S(1)}, f32[4,256]{1,0:T(4,128)S(1)}, u32[]{:S(2)}, u32[]{:S(2)}) collective-permute-start(f32[4,256]{1,0:T(4,128)S(1)} %get-tuple-element.72), channel_id=1, source_target_pairs={{0,16},{1,17},{2,18},{3,19},{4,20},{5,21},{6,22},{7,23},{8,24},{9,... | collective-permute-start | bytes 12296 | tf_op jit(solution)/shard_map/ppermute | solution.py:449
  25.6 1.9 %shard_map.152.refs_3_ = f32[3,1024]{1,0:T(4,128)S(1)} custom-call(f32[3,1024]{1,0:T(4,128)S(1)} %get-tuple-element.67.refs_0_, s32[2,8,128]{2,1,0:T(8,128)S(1)} %get-tuple-element.50.refs_1_, f32[1,8,128]{2,1,0:T(8,128)S(1)} %get-tuple-element.51.refs_2_, bf16[1024,1024]{1,0:T(8,128)(2,1)S(1)} %get-tuple-element.61.refs_3_), custom_call_target="tpu_custom_call" | custom-call | flops 2000000000 | bytes 100000 | tf_op jit(solution)/shard_map/pallas_call | solution.py:396
  27.6 0.9 %collective-permute-done.13.refs_7_ = f32[4,256]{1,0:T(4,128)S(1)} collective-permute-done((f32[4,256]{1,0:T(4,128)S(1)}, f32[4,256]{1,0:T(4,128)S(1)}, u32[]{:S(2)}, u32[]{:S(2)}) %collective-permute-start.13) | collective-permute-done | bytes 4128 | tf_op jit(solution)/shard_map/ppermute | solution.py:449
  28.5 2.1 %shard_map.153 = (f32[3,1024]{1,0:T(4,128)S(1)}, f32[3,1024]{1,0:T(4,128)S(1)}, f32[4,256]{1,0:T(4,128)S(1)}, f32[4,256]{1,0:T(4,128)S(1)}, f32[4,256]{1,0:T(4,1...) custom-call(f32[3,1024]{1,0:T(4,128)S(1)} %get-tuple-element.67.refs_0_, f32[3,1024]{1,0:T(4,128)S(1)} %get-tuple-element.68.refs_1_, ...), custom_call_target="tpu_custom_call" | custom-call | flops 1000000000 | bytes 100000 | tf_op jit(solution)/shard_map/pallas_call | solution.py:396
  30.6 1.9 %shard_map.154.refs_3_ = f32[3,1024]{1,0:T(4,128)S(1)} custom-call(f32[3,1024]{1,0:T(4,128)S(1)} %get-tuple-element.75.refs_0_.x_ref, s32[2,8,128]{2,1,0:T(8,128)S(1)} %get-tuple-element.50.refs_1_, f32[1,8,128]{2,1,0:T(8,128)S(1)} %get-tuple-element.51.refs_2_, bf16[1024,1024]{1,0:T(8,128)(2,1)S(1)} %get-tuple-element.61.refs_3_), custom_call_target="tpu_custom_call" | custom-call | flops 2000000000 | bytes 100000 | tf_op jit(solution)/shard_map/pallas_call | solution.py:396
  32.5 0.5 %collective-permute-start.15 = (f32[4,256]{1,0:T(4,128)S(1)}, f32[4,256]{1,0:T(4,128)S(1)}, u32[]{:S(2)}, u32[]{:S(2)}) collective-permute-start(f32[4,256]{1,0:T(4,128)S(1)} %get-tuple-element.77), channel_id=1, source_target_pairs={{0,1},{1,0},{2,3},{3,2},{4,5},{5,4},{6,7},{7,6},{8,9},{9,8},{10,11... | collective-permute-start | bytes 12296 | tf_op jit(solution)/shard_map/ppermute | solution.py:449
  33.2 1.2 %collective-permute-start.17 = (f32[4,256]{1,0:T(4,128)S(1)}, f32[4,256]{1,0:T(4,128)S(1)}, u32[]{:S(2)}, u32[]{:S(2)}) collective-permute-start(f32[4,256]{1,0:T(4,128)S(1)} %get-tuple-element.79), channel_id=1, source_target_pairs={{0,12},{1,13},{2,14},{3,15},{4,8},{5,9},{6,10},{7,11},{8,4},{9,5},... | collective-permute-start | bytes 12296 | tf_op jit(solution)/shard_map/ppermute | solution.py:449
  34.4 0.8 %collective-permute-start.18 = (f32[4,256]{1,0:T(4,128)S(1)}, f32[4,256]{1,0:T(4,128)S(1)}, u32[]{:S(2)}, u32[]{:S(2)}) collective-permute-start(f32[4,256]{1,0:T(4,128)S(1)} %get-tuple-element.80), channel_id=1, source_target_pairs={{0,16},{1,17},{2,18},{3,19},{4,20},{5,21},{6,22},{7,23},{8,24},{9,... | collective-permute-start | bytes 12296 | tf_op jit(solution)/shard_map/ppermute | solution.py:449
  35.2 2.1 %shard_map.156 = (f32[3,1024]{1,0:T(4,128)S(1)}, f32[8,32]{1,0:T(8,128)S(1)}) custom-call(f32[3,1024]{1,0:T(4,128)S(1)} %get-tuple-element.75.refs_0_.x_ref, f32[1,1024]{1,0:T(1,128)S(1)} %get-tuple-element.74.refs_10_.charge_ref.refs_3_, s32[1,96]{1,0:T(1,128)S(1)} %get-tuple-element.83.own_ref, s32[1,96]{1,0:T(1,128)S(1)} %get-tuple-element.84.partner_ref, ...), custom_call_target="tpu_custom_call" | custom-call | flops 2000000000 | bytes 100000 | tf_op jit(solution)/shard_map/pallas_call | solution.py:396
  37.4 0.7 %collective-permute-done.18.refs_7_.refs_11_ = f32[4,256]{1,0:T(4,128)S(1)} collective-permute-done((f32[4,256]{1,0:T(4,128)S(1)}, f32[4,256]{1,0:T(4,128)S(1)}, u32[]{:S(2)}, u32[]{:S(2)}) %collective-permute-start.18) | collective-permute-done | bytes 4128 | tf_op jit(solution)/shard_map/ppermute | solution.py:449
  38.0 1.8 %shard_map.155 = (f32[3,1024]{1,0:T(4,128)S(1)}, f32[3,1024]{1,0:T(4,128)S(1)}) custom-call(f32[3,1024]{1,0:T(4,128)S(1)} %get-tuple-element.75.refs_0_.x_ref, f32[3,1024]{1,0:T(4,128)S(1)} %get-tuple-element.76.refs_1_, f32[1,1024]{1,0:T(1,128)S(1)} %get-tuple-element.49.refs_2_, f32[3,1024]{1,0:T(4,128)S(1)} %shard_map.154.refs_3_, ...), custom_call_target="tpu_custom_call" | custom-call | flops 1000000000 | bytes 100000 | tf_op jit(solution)/shard_map/pallas_call | solution.py:396
  39.8 2.5 %shard_map.157 = (f32[3,1024]{1,0:T(4,128)}, f32[3,1024]{1,0:T(4,128)}, f32[3,1024]{1,0:T(4,128)}, f32[3,1024]{1,0:T(4,128)}) custom-call(f32[3,1024]{1,0:T(4,128)S(1)} %get-tuple-element.75.refs_0_.x_ref, f32[3,1024]{1,0:T(4,128)S(1)} %get-tuple-element.82.refs_1_, f32[1,1024]{1,0:T(1,128)S(1)} %get-tuple-element.49.refs_2_, ...), custom_call_target="tpu_custom_call" | custom-call | tf_op jit(solution)/shard_map/pallas_call | solution.py:481
  (27 shorter events, 1.0 us)
Async XLA Ops:
  2.9 9.1 %collective-permute-start = (f32[4,256]{1,0:T(4,128)S(1)}, f32[4,256]{1,0:T(4,128)S(1)}, u32[]{:S(2)}, u32[]{:S(2)}) collective-permute-start(f32[4,256]{1,0:T(4,128)S(1)} %get-tuple-element.53), channel_id=1, source_target_pairs={{0,1},{1,0},{2,3},{3,2},{4,5},{5,4},{6,7},{7,6},{8,9},{9,8},{10,11... | collective-permute-start | bytes 12296 | tf_op jit(solution)/shard_map/ppermute | solution.py:449
  6.0 6.0 %collective-permute-start.1 = (f32[4,256]{1,0:T(4,128)S(1)}, f32[4,256]{1,0:T(4,128)S(1)}, u32[]{:S(2)}, u32[]{:S(2)}) collective-permute-start(f32[4,256]{1,0:T(4,128)S(1)} %get-tuple-element.54), channel_id=1, source_target_pairs={{0,4},{1,2},{2,1},{3,7},{4,0},{5,6},{6,5},{7,3},{8,12},{9,10},{10,... | collective-permute-start | bytes 12296 | tf_op jit(solution)/shard_map/ppermute | solution.py:449
  6.0 6.0 %collective-permute-start.2 = (f32[4,256]{1,0:T(4,128)S(1)}, f32[4,256]{1,0:T(4,128)S(1)}, u32[]{:S(2)}, u32[]{:S(2)}) collective-permute-start(f32[4,256]{1,0:T(4,128)S(1)} %get-tuple-element.55), channel_id=1, source_target_pairs={{0,12},{1,13},{2,14},{3,15},{4,8},{5,9},{6,10},{7,11},{8,4},{9,5},... | collective-permute-start | bytes 12296 | tf_op jit(solution)/shard_map/ppermute | solution.py:449
  7.6 4.4 %collective-permute-start.3 = (f32[4,256]{1,0:T(4,128)S(1)}, f32[4,256]{1,0:T(4,128)S(1)}, u32[]{:S(2)}, u32[]{:S(2)}) collective-permute-start(f32[4,256]{1,0:T(4,128)S(1)} %get-tuple-element.56), channel_id=1, source_target_pairs={{0,16},{1,17},{2,18},{3,19},{4,20},{5,21},{6,22},{7,23},{8,24},{9,... | collective-permute-start | bytes 12296 | tf_op jit(solution)/shard_map/ppermute | solution.py:449
  9.1 2.9 %collective-permute-start.4 = (f32[4,256]{1,0:T(4,128)S(1)}, f32[4,256]{1,0:T(4,128)S(1)}, u32[]{:S(2)}, u32[]{:S(2)}) collective-permute-start(f32[4,256]{1,0:T(4,128)S(1)} %get-tuple-element.57), channel_id=1, source_target_pairs={{0,4},{1,5},{2,6},{3,7},{4,0},{5,1},{6,2},{7,3},{8,12},{9,13},{10,... | collective-permute-start | bytes 12296 | tf_op jit(solution)/shard_map/ppermute | solution.py:449
  14.0 6.1 %collective-permute-start.5 = (f32[4,256]{1,0:T(4,128)S(1)}, f32[4,256]{1,0:T(4,128)S(1)}, u32[]{:S(2)}, u32[]{:S(2)}) collective-permute-start(f32[4,256]{1,0:T(4,128)S(1)} %get-tuple-element.62), channel_id=1, source_target_pairs={{0,1},{1,0},{2,3},{3,2},{4,5},{5,4},{6,7},{7,6},{8,9},{9,8},{10,11... | collective-permute-start | bytes 12296 | tf_op jit(solution)/shard_map/ppermute | solution.py:449
  16.9 3.1 %collective-permute-start.6 = (f32[4,256]{1,0:T(4,128)S(1)}, f32[4,256]{1,0:T(4,128)S(1)}, u32[]{:S(2)}, u32[]{:S(2)}) collective-permute-start(f32[4,256]{1,0:T(4,128)S(1)} %get-tuple-element.63), channel_id=1, source_target_pairs={{0,4},{1,2},{2,1},{3,7},{4,0},{5,6},{6,5},{7,3},{8,12},{9,10},{10,... | collective-permute-start | bytes 12296 | tf_op jit(solution)/shard_map/ppermute | solution.py:449
  16.9 3.1 %collective-permute-start.7 = (f32[4,256]{1,0:T(4,128)S(1)}, f32[4,256]{1,0:T(4,128)S(1)}, u32[]{:S(2)}, u32[]{:S(2)}) collective-permute-start(f32[4,256]{1,0:T(4,128)S(1)} %get-tuple-element.64), channel_id=1, source_target_pairs={{0,12},{1,13},{2,14},{3,15},{4,8},{5,9},{6,10},{7,11},{8,4},{9,5},... | collective-permute-start | bytes 12296 | tf_op jit(solution)/shard_map/ppermute | solution.py:449
  17.5 3.6 %collective-permute-start.8 = (f32[4,256]{1,0:T(4,128)S(1)}, f32[4,256]{1,0:T(4,128)S(1)}, u32[]{:S(2)}, u32[]{:S(2)}) collective-permute-start(f32[4,256]{1,0:T(4,128)S(1)} %get-tuple-element.65), channel_id=1, source_target_pairs={{0,16},{1,17},{2,18},{3,19},{4,20},{5,21},{6,22},{7,23},{8,24},{9,... | collective-permute-start | bytes 12296 | tf_op jit(solution)/shard_map/ppermute | solution.py:449
  18.1 3.1 %collective-permute-start.9 = (f32[4,256]{1,0:T(4,128)S(1)}, f32[4,256]{1,0:T(4,128)S(1)}, u32[]{:S(2)}, u32[]{:S(2)}) collective-permute-start(f32[4,256]{1,0:T(4,128)S(1)} %get-tuple-element.66), channel_id=1, source_target_pairs={{0,4},{1,5},{2,6},{3,7},{4,0},{5,1},{6,2},{7,3},{8,12},{9,13},{10,... | collective-permute-start | bytes 12296 | tf_op jit(solution)/shard_map/ppermute | solution.py:449
  23.0 4.5 %collective-permute-start.10 = (f32[4,256]{1,0:T(4,128)S(1)}, f32[4,256]{1,0:T(4,128)S(1)}, u32[]{:S(2)}, u32[]{:S(2)}) collective-permute-start(f32[4,256]{1,0:T(4,128)S(1)} %get-tuple-element.69), channel_id=1, source_target_pairs={{0,1},{1,0},{2,3},{3,2},{4,5},{5,4},{6,7},{7,6},{8,9},{9,8},{10,11... | collective-permute-start | bytes 12296 | tf_op jit(solution)/shard_map/ppermute | solution.py:449
  23.3 4.3 %collective-permute-start.11 = (f32[4,256]{1,0:T(4,128)S(1)}, f32[4,256]{1,0:T(4,128)S(1)}, u32[]{:S(2)}, u32[]{:S(2)}) collective-permute-start(f32[4,256]{1,0:T(4,128)S(1)} %get-tuple-element.70), channel_id=1, source_target_pairs={{0,4},{1,2},{2,1},{3,7},{4,0},{5,6},{6,5},{7,3},{8,12},{9,10},{10,... | collective-permute-start | bytes 12296 | tf_op jit(solution)/shard_map/ppermute | solution.py:449
  23.3 4.3 %collective-permute-start.12 = (f32[4,256]{1,0:T(4,128)S(1)}, f32[4,256]{1,0:T(4,128)S(1)}, u32[]{:S(2)}, u32[]{:S(2)}) collective-permute-start(f32[4,256]{1,0:T(4,128)S(1)} %get-tuple-element.71), channel_id=1, source_target_pairs={{0,12},{1,13},{2,14},{3,15},{4,8},{5,9},{6,10},{7,11},{8,4},{9,5},... | collective-permute-start | bytes 12296 | tf_op jit(solution)/shard_map/ppermute | solution.py:449
  24.9 3.6 %collective-permute-start.13 = (f32[4,256]{1,0:T(4,128)S(1)}, f32[4,256]{1,0:T(4,128)S(1)}, u32[]{:S(2)}, u32[]{:S(2)}) collective-permute-start(f32[4,256]{1,0:T(4,128)S(1)} %get-tuple-element.72), channel_id=1, source_target_pairs={{0,16},{1,17},{2,18},{3,19},{4,20},{5,21},{6,22},{7,23},{8,24},{9,... | collective-permute-start | bytes 12296 | tf_op jit(solution)/shard_map/ppermute | solution.py:449
  25.6 2.9 %collective-permute-start.14 = (f32[4,256]{1,0:T(4,128)S(1)}, f32[4,256]{1,0:T(4,128)S(1)}, u32[]{:S(2)}, u32[]{:S(2)}) collective-permute-start(f32[4,256]{1,0:T(4,128)S(1)} %get-tuple-element.73), channel_id=1, source_target_pairs={{0,4},{1,5},{2,6},{3,7},{4,0},{5,1},{6,2},{7,3},{8,12},{9,13},{10,... | collective-permute-start | bytes 12296 | tf_op jit(solution)/shard_map/ppermute | solution.py:449
  32.5 4.8 %collective-permute-start.15 = (f32[4,256]{1,0:T(4,128)S(1)}, f32[4,256]{1,0:T(4,128)S(1)}, u32[]{:S(2)}, u32[]{:S(2)}) collective-permute-start(f32[4,256]{1,0:T(4,128)S(1)} %get-tuple-element.77), channel_id=1, source_target_pairs={{0,1},{1,0},{2,3},{3,2},{4,5},{5,4},{6,7},{7,6},{8,9},{9,8},{10,11... | collective-permute-start | bytes 12296 | tf_op jit(solution)/shard_map/ppermute | solution.py:449
  33.1 4.3 %collective-permute-start.16 = (f32[4,256]{1,0:T(4,128)S(1)}, f32[4,256]{1,0:T(4,128)S(1)}, u32[]{:S(2)}, u32[]{:S(2)}) collective-permute-start(f32[4,256]{1,0:T(4,128)S(1)} %get-tuple-element.78), channel_id=1, source_target_pairs={{0,4},{1,2},{2,1},{3,7},{4,0},{5,6},{6,5},{7,3},{8,12},{9,10},{10,... | collective-permute-start | bytes 12296 | tf_op jit(solution)/shard_map/ppermute | solution.py:449
  33.2 4.2 %collective-permute-start.17 = (f32[4,256]{1,0:T(4,128)S(1)}, f32[4,256]{1,0:T(4,128)S(1)}, u32[]{:S(2)}, u32[]{:S(2)}) collective-permute-start(f32[4,256]{1,0:T(4,128)S(1)} %get-tuple-element.79), channel_id=1, source_target_pairs={{0,12},{1,13},{2,14},{3,15},{4,8},{5,9},{6,10},{7,11},{8,4},{9,5},... | collective-permute-start | bytes 12296 | tf_op jit(solution)/shard_map/ppermute | solution.py:449
  34.4 3.6 %collective-permute-start.18 = (f32[4,256]{1,0:T(4,128)S(1)}, f32[4,256]{1,0:T(4,128)S(1)}, u32[]{:S(2)}, u32[]{:S(2)}) collective-permute-start(f32[4,256]{1,0:T(4,128)S(1)} %get-tuple-element.80), channel_id=1, source_target_pairs={{0,16},{1,17},{2,18},{3,19},{4,20},{5,21},{6,22},{7,23},{8,24},{9,... | collective-permute-start | bytes 12296 | tf_op jit(solution)/shard_map/ppermute | solution.py:449
  35.2 2.9 %collective-permute-start.19 = (f32[4,256]{1,0:T(4,128)S(1)}, f32[4,256]{1,0:T(4,128)S(1)}, u32[]{:S(2)}, u32[]{:S(2)}) collective-permute-start(f32[4,256]{1,0:T(4,128)S(1)} %get-tuple-element.81), channel_id=1, source_target_pairs={{0,4},{1,5},{2,6},{3,7},{4,0},{5,1},{6,2},{7,3},{8,12},{9,13},{10,... | collective-permute-start | bytes 12296 | tf_op jit(solution)/shard_map/ppermute | solution.py:449

commit v3 on v2

--- a/solution.py
+++ b/solution.py
@@ -18,7 +18,7 @@
 BLOCK = 256
 FAR = -1.0e6
 
-N_START = 12
+N_START = 10
 F32 = jnp.float32
 BF16 = jnp.bfloat16
 
@@ -164,12 +164,12 @@
 
 def start_kernel(swaps, *refs):
     sources, refs = refs[:N_START], refs[N_START:]
-    x_ref, mass_ref, charge_ref, own_ref, partner_ref, count_ref = refs[:6]
-    index_out, bonds_out, bond_k_out, x_out, v_out = refs[6:11]
-    send_refs, refs = refs[11 : 11 + len(swaps)], refs[11 + len(swaps) :]
+    x_ref, mass_ref, charge_ref, partner_ref = refs[:4]
+    index_out, bonds_out, bond_k_out, x_out, v_out = refs[4:9]
+    send_refs, refs = refs[9 : 9 + len(swaps)], refs[9 + len(swaps) :]
     v_ref, fast_ref, slow_ref, index_ref, bonds_ref, bond_k_ref, sems = refs
     kept = [x_ref, mass_ref, index_ref, v_ref, fast_ref, slow_ref]
-    kept += [charge_ref, bonds_ref, bond_k_ref, own_ref, partner_ref, count_ref]
+    kept += [charge_ref, bonds_ref, bond_k_ref, partner_ref]
     copies = [
         pltpu.make_async_copy(src, dst, sems.at[k]) for k, (src, dst) in enumerate(zip(sources, kept))
     ]
@@ -215,11 +215,11 @@
     return [a[:, s : s + width] for s in range(0, a.shape[1], width)]
 
 
-def tile_counts(own_ref, partner_ref, count_ref, n_tiles, swaps):
-    slots = own_ref.shape[1]
+def tile_counts(own_ref, partner_ref, n_tiles, swaps):
+    slots = partner_ref.shape[1]
     partner = partner_ref[...]
-    own = own_ref[...]
-    live = lax.broadcasted_iota(jnp.int32, (1, slots), 1) < count_ref[...]
+    own = own_ref[:, :slots]
+    live = lax.broadcasted_iota(jnp.int32, (1, slots), 1) < own_ref[:, slots:]
     outside = partner - n_tiles
     axis = lax.shift_right_logical(outside, 2)
     side = lax.bitwise_and(lax.shift_right_logical(outside, 1), 1)
@@ -263,12 +263,12 @@
     return (LONG_SCALE * LONG_UNIT) * charge * (u * part[3:4] - part)
 
 
-def slow_own_kernel(swaps, x_ref, charge_ref, own_ref, partner_ref, count_ref, slow_out, counts_out):
+def slow_own_kernel(swaps, x_ref, charge_ref, own_ref, partner_ref, slow_out, counts_out):
     n = x_ref.shape[1]
     charge = charge_ref[...]
     u = scaled(x_ref[...], centre((8, n)), LONG_UNIT)
     pair, _ = source_matrices(u)
-    counts = tile_counts(own_ref, partner_ref, count_ref, n // LANES, swaps)
+    counts = tile_counts(own_ref, partner_ref, n // LANES, swaps)
     counts_out[...] = counts
     sums = pair_sums(
         blocks(receiver_matrix(u)),
@@ -290,8 +290,6 @@
         pltpu.make_async_copy(src, dst, sems.at[k])
         for k, (src, dst) in enumerate(zip([moved, v_new, force_ref, slow_new], outs))
     ]
-    copies[0].start()
-    copies[2].start()
     u = scaled(x, centre((8, n)), LONG_UNIT)
     charge = charge_ref[...]
     sources, totals = [], []
@@ -306,8 +304,8 @@
     slow = slow_ref[...] + slow_from(u, charge, jnp.concatenate(sums, axis=1))[:3]
     slow_new[...] = slow
     v_new[...] = v_ref[...] + (0.5 * INNER * STEP) * mass_ref[...] * slow
-    copies[1].start()
-    copies[3].start()
+    for c in copies:
+        c.start()
     for c in copies:
         c.wait()
 
@@ -392,6 +390,23 @@
     write_faces(x, index_ref, refs[2:])
 
 
+def own_last_kernel(swaps, *refs):
+    own_kernel(False, *refs[:4], refs[7])
+    slow_own_kernel(swaps, refs[0], *refs[4:7], *refs[8:])
+
+
+def halo_last_kernel(swaps, *refs):
+    x_ref, v_ref, mass_ref, force_ref = refs[:4]
+    arrived, refs = refs[4 : 4 + len(swaps)], refs[4 + len(swaps) :]
+    charge_ref, counts_ref, slow_ref, start_ref = refs[:4]
+    outs, (moved, v_new, slow_new, force_new, v_mid, sems) = refs[4:8], refs[8:]
+    halo_kernel(swaps, True, False, x_ref, v_ref, mass_ref, force_ref, *arrived, force_new, v_mid)
+    slow_halo_kernel(
+        swaps, x_ref, v_mid, mass_ref, charge_ref, counts_ref, slow_ref, force_new, start_ref, *arrived, *outs,
+        moved, v_new, slow_new, sems,
+    )
+
+
 def call(kernel, outs, args, flops=0):
     return pl.pallas_call(
         kernel,
@@ -423,9 +438,9 @@
     sends = [((4, halo_index.shape[1]), F32)] * len(swaps)
     start_args = [positions, inv_mass.reshape(1, n), halo_index, velocities, fast_force, slow_force]
     start_args += [charge.reshape(1, n), bonds, bond_k.reshape(1, -1)]
-    start_args += [pair_own.reshape(1, -1), pair_partner.reshape(1, -1), pair_count.reshape(1, 1)]
+    start_args.append(pair_partner.reshape(1, -1))
     assert len(start_args) == N_START
-    kept = [(start_args[k].shape, start_args[k].dtype) for k in (0, 1, 6, 9, 10, 11)]
+    kept = [(start_args[k].shape, start_args[k].dtype) for k in (0, 1, 6, 9)]
     n_bonds = bonds.shape[1]
     face_rows = len(swaps) * halo_index.shape[1] // LANES
     kept.append(((-(-face_rows // 8) * 8, LANES), jnp.int32))
@@ -434,8 +449,8 @@
     scratch = [pltpu.VMEM((3, n), F32)] * 3
     scratch += [pltpu.VMEM(halo_index.shape, jnp.int32), pltpu.VMEM(bonds.shape, jnp.int32)]
     scratch += [pltpu.VMEM((1, n_bonds), F32), pltpu.SemaphoreType.DMA((N_START,))]
-    start_args = [pltpu.with_memory_space_constraint(a, pltpu.HBM) for a in start_args[:-1]] + start_args[-1:]
-    start, mass, charge, own, partner, count, index, bonds, bond_k, x, v, *faces = pl.pallas_call(
+    start_args = [pltpu.with_memory_space_constraint(a, pltpu.HBM) for a in start_args]
+    start, mass, charge, partner, index, bonds, bond_k, x, v, *faces = pl.pallas_call(
         functools.partial(start_kernel, swaps),
         out_shape=[jax.ShapeDtypeStruct(s, d) for s, d in kept + [vec, vec] + sends],
         in_specs=[pl.BlockSpec(memory_space=pltpu.HBM)] * N_START,
@@ -452,21 +467,19 @@
             outs.append(((n_bonds, n), BF16))
         else:
             args.append(incidence)
+        if last:
+            own = jnp.concatenate([pair_own, pair_count]).reshape(1, -1)
+            force, slow, counts = call(
+                functools.partial(own_last_kernel, swaps),
+                [vec, vec, ((8, 32), F32)],
+                args + [charge, own, partner],
+                flops=4 * 10**9,
+            )
+            break
         force, *built = call(functools.partial(own_kernel, first), outs, args, flops=2 * 10**9)
         if first:
             incidence = built[0]
         args = [x, v, mass, force] + arrived
-        if last:
-            slow, counts = call(
-                functools.partial(slow_own_kernel, swaps),
-                [vec, ((8, 32), F32)],
-                [x, charge, own, partner, count],
-                flops=2 * 10**9,
-            )
-            force, v = call(
-                functools.partial(halo_kernel, swaps, True, False), [vec, vec], args, flops=10**9
-            )
-            break
         args.append(index)
         send_charge = turn == INNER - 2
         if send_charge:
@@ -477,13 +490,13 @@
             args,
             flops=10**9,
         )
-    args = [x, v, mass, charge, counts, slow, force, start] + arrived
+    args = [x, v, mass, force] + arrived + [charge, counts, slow, start]
     return pl.pallas_call(
-        functools.partial(slow_halo_kernel, swaps),
+        functools.partial(halo_last_kernel, swaps),
         out_shape=[jax.ShapeDtypeStruct(*vec)] * 4,
         in_specs=[pl.BlockSpec(memory_space=pltpu.VMEM)] * len(args),
         out_specs=[pl.BlockSpec(memory_space=pltpu.HBM)] * 4,
-        scratch_shapes=[pltpu.VMEM((3, n), F32)] * 3 + [pltpu.SemaphoreType.DMA((4,))],
+        scratch_shapes=[pltpu.VMEM((3, n), F32)] * 5 + [pltpu.SemaphoreType.DMA((4,))],
         compiler_params=pltpu.CompilerParams(vmem_limit_bytes=24 * 1024 * 1024),
     )(*args)
 

time: 42.8 us -> 40.5 us (0.946)
  Pallas kernels: 22.6 us -> 20.8 us
  waiting for transfers between devices: 2.74 us -> 2.06 us
    pallas_call x9 -> x7, Pallas kernels: 18.5 us -> 15.9 us  [call(): pl.pallas_call(kernel, out_shape=[jax.ShapeDtypeStruct(s, d) for s, d in...]
    pallas_call x1, Pallas kernels: 2.48 us -> 3.86 us  [on_device(): pl.pallas_call(functools.partial(halo_last_kernel, swaps), out_shape=[jax...]
    ppermute x20, waiting for transfers between devices: 2.74 us -> 2.06 us  [on_device(): lax.ppermute(f, AXES, perm)]
    pallas_call x1, Pallas kernels: 1.61 us -> 1.07 us  [on_device(): pl.pallas_call(functools.partial(start_kernel, swaps), out_shape=[jax.Sha...]
  transfers between devices with their start and end apart: 20 -> 20, of which waited for: 3 -> 2; matrix products, arithmetic and copies ran while one was open for 0% -> 0% of each run, Pallas kernels for 21% -> 25%
where the time goes in v3:
time: 40.5 us; the launch traced here: 40.2 us
  Pallas kernels  20.8 us (51%)
  starting transfers between devices  15.6 us (39%)
  waiting for transfers between devices  2.06 us (5%)
  between operations  1.63 us (4%)
    pallas_call x7, Pallas kernels, call(): pl.pallas_call(kernel, out_shape=[jax.ShapeDtypeStruct(s, d) for s, d in...  15.9 us
    ppermute x20, starting transfers between devices, on_device(): lax.ppermute(f, AXES, perm)  15.6 us
    pallas_call x1, Pallas kernels, on_device(): pl.pallas_call(functools.partial(halo_last_kernel, swaps), out_shape=[jax...  3.86 us
    ppermute x20, waiting for transfers between devices, on_device(): lax.ppermute(f, AXES, perm)  2.06 us
    pallas_call x1, Pallas kernels, on_device(): pl.pallas_call(functools.partial(start_kernel, swaps), out_shape=[jax.Sha...  1.07 us
  transfers between devices with their start and end apart: 20, of which 2 were waited for; matrix products, arithmetic and copies ran while one was open for 0% of the time, Pallas kernels for 25%

profile of v3, /device:TPU:0, one launch (start us, length us, event | category | flops | bytes accessed | tf_op | source)
XLA Modules:
  0.0 40.2 jit_solution(10586948521588721211)
XLA Ops:
  0.6 1.1 %shard_map.147 = (f32[3,1024]{1,0:T(4,128)S(1)}, f32[1,1024]{1,0:T(1,128)S(1)}, f32[1,1024]{1,0:T(1,128)S(1)}, s32[1,96]{1,0:T(1,128)S(1)}, s32[16,128]{1,0:T(8,...) custom-call(f32[3,1024]{1,0:T(4,128)} %refs_0_.1, ...), custom_call_target="tpu_custom_call" | custom-call | tf_op jit(solution)/shard_map/pallas_call | solution.py:453
  1.7 3.1 %collective-permute-start = (f32[4,256]{1,0:T(4,128)S(1)}, f32[4,256]{1,0:T(4,128)S(1)}, u32[]{:S(2)}, u32[]{:S(2)}) collective-permute-start(f32[4,256]{1,0:T(4,128)S(1)} %get-tuple-element.50), channel_id=1, source_target_pairs={{0,1},{1,0},{2,3},{3,2},{4,5},{5,4},{6,7},{7,6},{8,9},{9,8},{10,11... | collective-permute-start | bytes 12296 | tf_op jit(solution)/shard_map/ppermute | solution.py:464
  4.8 1.6 %collective-permute-start.2 = (f32[4,256]{1,0:T(4,128)S(1)}, f32[4,256]{1,0:T(4,128)S(1)}, u32[]{:S(2)}, u32[]{:S(2)}) collective-permute-start(f32[4,256]{1,0:T(4,128)S(1)} %get-tuple-element.52), channel_id=1, source_target_pairs={{0,12},{1,13},{2,14},{3,15},{4,8},{5,9},{6,10},{7,11},{8,4},{9,5},... | collective-permute-start | bytes 12296 | tf_op jit(solution)/shard_map/ppermute | solution.py:464
  6.5 1.5 %collective-permute-start.3 = (f32[4,256]{1,0:T(4,128)S(1)}, f32[4,256]{1,0:T(4,128)S(1)}, u32[]{:S(2)}, u32[]{:S(2)}) collective-permute-start(f32[4,256]{1,0:T(4,128)S(1)} %get-tuple-element.53), channel_id=1, source_target_pairs={{0,16},{1,17},{2,18},{3,19},{4,20},{5,21},{6,22},{7,23},{8,24},{9,... | collective-permute-start | bytes 12296 | tf_op jit(solution)/shard_map/ppermute | solution.py:464
  8.6 2.8 %shard_map.148 = (f32[3,1024]{1,0:T(4,128)S(1)}, bf16[1024,1024]{1,0:T(8,128)(2,1)S(1)}) custom-call(f32[3,1024]{1,0:T(4,128)S(1)} %get-tuple-element.44.refs_0_, s32[2,8,128]{2,1,0:T(8,128)S(1)} %get-tuple-element.47.refs_1_, f32[1,8,128]{2,1,0:T(8,128)S(1)} %get-tuple-element.48.refs_2_), custom_call_target="tpu_custom_call" | custom-call | flops 2000000000 | bytes 100000 | tf_op jit(solution)/shard_map/pallas_call | solution.py:411
  11.6 1.9 %shard_map.149 = (f32[3,1024]{1,0:T(4,128)S(1)}, f32[3,1024]{1,0:T(4,128)S(1)}, f32[4,256]{1,0:T(4,128)S(1)}, f32[4,256]{1,0:T(4,128)S(1)}, f32[4,256]{1,0:T(4,1...) custom-call(f32[3,1024]{1,0:T(4,128)S(1)} %get-tuple-element.44.refs_0_, f32[3,1024]{1,0:T(4,128)S(1)} %get-tuple-element.45.refs_1_, ...), custom_call_target="tpu_custom_call" | custom-call | flops 1000000000 | bytes 100000 | tf_op jit(solution)/shard_map/pallas_call | solution.py:411
  13.5 2.9 %collective-permute-start.5 = (f32[4,256]{1,0:T(4,128)S(1)}, f32[4,256]{1,0:T(4,128)S(1)}, u32[]{:S(2)}, u32[]{:S(2)}) collective-permute-start(f32[4,256]{1,0:T(4,128)S(1)} %get-tuple-element.59), channel_id=1, source_target_pairs={{0,1},{1,0},{2,3},{3,2},{4,5},{5,4},{6,7},{7,6},{8,9},{9,8},{10,11... | collective-permute-start | bytes 12296 | tf_op jit(solution)/shard_map/ppermute | solution.py:464
  16.5 0.6 %collective-permute-start.7 = (f32[4,256]{1,0:T(4,128)S(1)}, f32[4,256]{1,0:T(4,128)S(1)}, u32[]{:S(2)}, u32[]{:S(2)}) collective-permute-start(f32[4,256]{1,0:T(4,128)S(1)} %get-tuple-element.61), channel_id=1, source_target_pairs={{0,12},{1,13},{2,14},{3,15},{4,8},{5,9},{6,10},{7,11},{8,4},{9,5},... | collective-permute-start | bytes 12296 | tf_op jit(solution)/shard_map/ppermute | solution.py:464
  17.1 0.5 %collective-permute-start.8 = (f32[4,256]{1,0:T(4,128)S(1)}, f32[4,256]{1,0:T(4,128)S(1)}, u32[]{:S(2)}, u32[]{:S(2)}) collective-permute-start(f32[4,256]{1,0:T(4,128)S(1)} %get-tuple-element.62), channel_id=1, source_target_pairs={{0,16},{1,17},{2,18},{3,19},{4,20},{5,21},{6,22},{7,23},{8,24},{9,... | collective-permute-start | bytes 12296 | tf_op jit(solution)/shard_map/ppermute | solution.py:464
  17.6 1.9 %shard_map.150.refs_3_ = f32[3,1024]{1,0:T(4,128)S(1)} custom-call(f32[3,1024]{1,0:T(4,128)S(1)} %get-tuple-element.56.refs_0_, s32[2,8,128]{2,1,0:T(8,128)S(1)} %get-tuple-element.47.refs_1_, f32[1,8,128]{2,1,0:T(8,128)S(1)} %get-tuple-element.48.refs_2_, bf16[1024,1024]{1,0:T(8,128)(2,1)S(1)} %get-tuple-element.58.refs_3_), custom_call_target="tpu_custom_call" | custom-call | flops 2000000000 | bytes 100000 | tf_op jit(solution)/shard_map/pallas_call | solution.py:411
  19.6 1.1 %collective-permute-done.8.refs_7_ = f32[4,256]{1,0:T(4,128)S(1)} collective-permute-done((f32[4,256]{1,0:T(4,128)S(1)}, f32[4,256]{1,0:T(4,128)S(1)}, u32[]{:S(2)}, u32[]{:S(2)}) %collective-permute-start.8) | collective-permute-done | bytes 4128 | tf_op jit(solution)/shard_map/ppermute | solution.py:464
  20.7 1.9 %shard_map.151 = (f32[3,1024]{1,0:T(4,128)S(1)}, f32[3,1024]{1,0:T(4,128)S(1)}, f32[4,256]{1,0:T(4,128)S(1)}, f32[4,256]{1,0:T(4,128)S(1)}, f32[4,256]{1,0:T(4,1...) custom-call(f32[3,1024]{1,0:T(4,128)S(1)} %get-tuple-element.56.refs_0_, f32[3,1024]{1,0:T(4,128)S(1)} %get-tuple-element.57.refs_1_, ...), custom_call_target="tpu_custom_call" | custom-call | flops 1000000000 | bytes 100000 | tf_op jit(solution)/shard_map/pallas_call | solution.py:411
  22.6 0.2 collective-permute-start.10
  22.8 1.6 %collective-permute-start.12 = (f32[4,256]{1,0:T(4,128)S(1)}, f32[4,256]{1,0:T(4,128)S(1)}, u32[]{:S(2)}, u32[]{:S(2)}) collective-permute-start(f32[4,256]{1,0:T(4,128)S(1)} %get-tuple-element.68), channel_id=1, source_target_pairs={{0,12},{1,13},{2,14},{3,15},{4,8},{5,9},{6,10},{7,11},{8,4},{9,5},... | collective-permute-start | bytes 12296 | tf_op jit(solution)/shard_map/ppermute | solution.py:464
  24.5 0.7 %collective-permute-start.13 = (f32[4,256]{1,0:T(4,128)S(1)}, f32[4,256]{1,0:T(4,128)S(1)}, u32[]{:S(2)}, u32[]{:S(2)}) collective-permute-start(f32[4,256]{1,0:T(4,128)S(1)} %get-tuple-element.69), channel_id=1, source_target_pairs={{0,16},{1,17},{2,18},{3,19},{4,20},{5,21},{6,22},{7,23},{8,24},{9,... | collective-permute-start | bytes 12296 | tf_op jit(solution)/shard_map/ppermute | solution.py:464
  25.2 1.9 %shard_map.152.refs_3_ = f32[3,1024]{1,0:T(4,128)S(1)} custom-call(f32[3,1024]{1,0:T(4,128)S(1)} %get-tuple-element.64.refs_0_, s32[2,8,128]{2,1,0:T(8,128)S(1)} %get-tuple-element.47.refs_1_, f32[1,8,128]{2,1,0:T(8,128)S(1)} %get-tuple-element.48.refs_2_, bf16[1024,1024]{1,0:T(8,128)(2,1)S(1)} %get-tuple-element.58.refs_3_), custom_call_target="tpu_custom_call" | custom-call | flops 2000000000 | bytes 100000 | tf_op jit(solution)/shard_map/pallas_call | solution.py:411
  27.2 0.9 %collective-permute-done.13.refs_7_ = f32[4,256]{1,0:T(4,128)S(1)} collective-permute-done((f32[4,256]{1,0:T(4,128)S(1)}, f32[4,256]{1,0:T(4,128)S(1)}, u32[]{:S(2)}, u32[]{:S(2)}) %collective-permute-start.13) | collective-permute-done | bytes 4128 | tf_op jit(solution)/shard_map/ppermute | solution.py:464
  28.1 2.1 %shard_map.153 = (f32[3,1024]{1,0:T(4,128)S(1)}, f32[3,1024]{1,0:T(4,128)S(1)}, f32[4,256]{1,0:T(4,128)S(1)}, f32[4,256]{1,0:T(4,128)S(1)}, f32[4,256]{1,0:T(4,1...) custom-call(f32[3,1024]{1,0:T(4,128)S(1)} %get-tuple-element.64.refs_0_, f32[3,1024]{1,0:T(4,128)S(1)} %get-tuple-element.65.refs_1_, ...), custom_call_target="tpu_custom_call" | custom-call | flops 1000000000 | bytes 100000 | tf_op jit(solution)/shard_map/pallas_call | solution.py:411
  30.2 0.6 %collective-permute-start.15 = (f32[4,256]{1,0:T(4,128)S(1)}, f32[4,256]{1,0:T(4,128)S(1)}, u32[]{:S(2)}, u32[]{:S(2)}) collective-permute-start(f32[4,256]{1,0:T(4,128)S(1)} %get-tuple-element.76), channel_id=1, source_target_pairs={{0,1},{1,0},{2,3},{3,2},{4,5},{5,4},{6,7},{7,6},{8,9},{9,8},{10,11... | collective-permute-start | bytes 12296 | tf_op jit(solution)/shard_map/ppermute | solution.py:464
  30.7 0.1 collective-permute-start.16
  30.9 1.2 %collective-permute-start.17 = (f32[4,256]{1,0:T(4,128)S(1)}, f32[4,256]{1,0:T(4,128)S(1)}, u32[]{:S(2)}, u32[]{:S(2)}) collective-permute-start(f32[4,256]{1,0:T(4,128)S(1)} %get-tuple-element.78), channel_id=1, source_target_pairs={{0,12},{1,13},{2,14},{3,15},{4,8},{5,9},{6,10},{7,11},{8,4},{9,5},... | collective-permute-start | bytes 12296 | tf_op jit(solution)/shard_map/ppermute | solution.py:464
  32.1 0.8 %collective-permute-start.18 = (f32[4,256]{1,0:T(4,128)S(1)}, f32[4,256]{1,0:T(4,128)S(1)}, u32[]{:S(2)}, u32[]{:S(2)}) collective-permute-start(f32[4,256]{1,0:T(4,128)S(1)} %get-tuple-element.79), channel_id=1, source_target_pairs={{0,16},{1,17},{2,18},{3,19},{4,20},{5,21},{6,22},{7,23},{8,24},{9,... | collective-permute-start | bytes 12296 | tf_op jit(solution)/shard_map/ppermute | solution.py:464
  32.9 3.3 %shard_map.154 = (f32[3,1024]{1,0:T(4,128)S(1)}, f32[3,1024]{1,0:T(4,128)S(1)}, f32[8,32]{1,0:T(8,128)S(1)}) custom-call(f32[3,1024]{1,0:T(4,128)S(1)} %get-tuple-element.72.refs_0_, s32[2,8,128]{2,1,0:T(8,128)S(1)} %get-tuple-element.47.refs_1_, f32[1,8,128]{2,1,0:T(8,128)S(1)} %get-tuple-element.48.refs_2_, ...), custom_call_target="tpu_custom_call" | custom-call | flops 4000000000 | bytes 100000 | tf_op jit(solution)/shard_map/pallas_call | solution.py:411
  36.2 3.9 %shard_map.155 = (f32[3,1024]{1,0:T(4,128)}, f32[3,1024]{1,0:T(4,128)}, f32[3,1024]{1,0:T(4,128)}, f32[3,1024]{1,0:T(4,128)}) custom-call(f32[3,1024]{1,0:T(4,128)S(1)} %get-tuple-element.72.refs_0_, f32[3,1024]{1,0:T(4,128)S(1)} %get-tuple-element.73.refs_1_, f32[1,1024]{1,0:T(1,128)S(1)} %get-tuple-element.46.refs_2_, ...), custom_call_target="tpu_custom_call" | custom-call | tf_op jit(solution)/shard_map/pallas_call | solution.py:494
  (28 shorter events, 0.2 us)
Async XLA Ops:
  1.7 9.9 %collective-permute-start = (f32[4,256]{1,0:T(4,128)S(1)}, f32[4,256]{1,0:T(4,128)S(1)}, u32[]{:S(2)}, u32[]{:S(2)}) collective-permute-start(f32[4,256]{1,0:T(4,128)S(1)} %get-tuple-element.50), channel_id=1, source_target_pairs={{0,1},{1,0},{2,3},{3,2},{4,5},{5,4},{6,7},{7,6},{8,9},{9,8},{10,11... | collective-permute-start | bytes 12296 | tf_op jit(solution)/shard_map/ppermute | solution.py:464
  4.8 6.7 %collective-permute-start.1 = (f32[4,256]{1,0:T(4,128)S(1)}, f32[4,256]{1,0:T(4,128)S(1)}, u32[]{:S(2)}, u32[]{:S(2)}) collective-permute-start(f32[4,256]{1,0:T(4,128)S(1)} %get-tuple-element.51), channel_id=1, source_target_pairs={{0,4},{1,2},{2,1},{3,7},{4,0},{5,6},{6,5},{7,3},{8,12},{9,10},{10,... | collective-permute-start | bytes 12296 | tf_op jit(solution)/shard_map/ppermute | solution.py:464
  4.8 6.7 %collective-permute-start.2 = (f32[4,256]{1,0:T(4,128)S(1)}, f32[4,256]{1,0:T(4,128)S(1)}, u32[]{:S(2)}, u32[]{:S(2)}) collective-permute-start(f32[4,256]{1,0:T(4,128)S(1)} %get-tuple-element.52), channel_id=1, source_target_pairs={{0,12},{1,13},{2,14},{3,15},{4,8},{5,9},{6,10},{7,11},{8,4},{9,5},... | collective-permute-start | bytes 12296 | tf_op jit(solution)/shard_map/ppermute | solution.py:464
  6.5 5.1 %collective-permute-start.3 = (f32[4,256]{1,0:T(4,128)S(1)}, f32[4,256]{1,0:T(4,128)S(1)}, u32[]{:S(2)}, u32[]{:S(2)}) collective-permute-start(f32[4,256]{1,0:T(4,128)S(1)} %get-tuple-element.53), channel_id=1, source_target_pairs={{0,16},{1,17},{2,18},{3,19},{4,20},{5,21},{6,22},{7,23},{8,24},{9,... | collective-permute-start | bytes 12296 | tf_op jit(solution)/shard_map/ppermute | solution.py:464
  8.0 3.6 %collective-permute-start.4 = (f32[4,256]{1,0:T(4,128)S(1)}, f32[4,256]{1,0:T(4,128)S(1)}, u32[]{:S(2)}, u32[]{:S(2)}) collective-permute-start(f32[4,256]{1,0:T(4,128)S(1)} %get-tuple-element.54), channel_id=1, source_target_pairs={{0,4},{1,5},{2,6},{3,7},{4,0},{5,1},{6,2},{7,3},{8,12},{9,13},{10,... | collective-permute-start | bytes 12296 | tf_op jit(solution)/shard_map/ppermute | solution.py:464
  8.6 2.9 %copy-start = (s32[96]{0:T(128)S(1)}, s32[96]{0:T(128)}, u32[]{:S(2)}) copy-start(s32[96]{0:T(128)} %param.21) | copy-start | bytes 1156
  13.5 6.1 %collective-permute-start.5 = (f32[4,256]{1,0:T(4,128)S(1)}, f32[4,256]{1,0:T(4,128)S(1)}, u32[]{:S(2)}, u32[]{:S(2)}) collective-permute-start(f32[4,256]{1,0:T(4,128)S(1)} %get-tuple-element.59), channel_id=1, source_target_pairs={{0,1},{1,0},{2,3},{3,2},{4,5},{5,4},{6,7},{7,6},{8,9},{9,8},{10,11... | collective-permute-start | bytes 12296 | tf_op jit(solution)/shard_map/ppermute | solution.py:464
  16.5 3.1 %collective-permute-start.6 = (f32[4,256]{1,0:T(4,128)S(1)}, f32[4,256]{1,0:T(4,128)S(1)}, u32[]{:S(2)}, u32[]{:S(2)}) collective-permute-start(f32[4,256]{1,0:T(4,128)S(1)} %get-tuple-element.60), channel_id=1, source_target_pairs={{0,4},{1,2},{2,1},{3,7},{4,0},{5,6},{6,5},{7,3},{8,12},{9,10},{10,... | collective-permute-start | bytes 12296 | tf_op jit(solution)/shard_map/ppermute | solution.py:464
  16.5 3.1 %collective-permute-start.7 = (f32[4,256]{1,0:T(4,128)S(1)}, f32[4,256]{1,0:T(4,128)S(1)}, u32[]{:S(2)}, u32[]{:S(2)}) collective-permute-start(f32[4,256]{1,0:T(4,128)S(1)} %get-tuple-element.61), channel_id=1, source_target_pairs={{0,12},{1,13},{2,14},{3,15},{4,8},{5,9},{6,10},{7,11},{8,4},{9,5},... | collective-permute-start | bytes 12296 | tf_op jit(solution)/shard_map/ppermute | solution.py:464
  17.1 3.6 %collective-permute-start.8 = (f32[4,256]{1,0:T(4,128)S(1)}, f32[4,256]{1,0:T(4,128)S(1)}, u32[]{:S(2)}, u32[]{:S(2)}) collective-permute-start(f32[4,256]{1,0:T(4,128)S(1)} %get-tuple-element.62), channel_id=1, source_target_pairs={{0,16},{1,17},{2,18},{3,19},{4,20},{5,21},{6,22},{7,23},{8,24},{9,... | collective-permute-start | bytes 12296 | tf_op jit(solution)/shard_map/ppermute | solution.py:464
  17.6 3.1 %collective-permute-start.9 = (f32[4,256]{1,0:T(4,128)S(1)}, f32[4,256]{1,0:T(4,128)S(1)}, u32[]{:S(2)}, u32[]{:S(2)}) collective-permute-start(f32[4,256]{1,0:T(4,128)S(1)} %get-tuple-element.63), channel_id=1, source_target_pairs={{0,4},{1,5},{2,6},{3,7},{4,0},{5,1},{6,2},{7,3},{8,12},{9,13},{10,... | collective-permute-start | bytes 12296 | tf_op jit(solution)/shard_map/ppermute | solution.py:464
  22.6 4.5 %collective-permute-start.10 = (f32[4,256]{1,0:T(4,128)S(1)}, f32[4,256]{1,0:T(4,128)S(1)}, u32[]{:S(2)}, u32[]{:S(2)}) collective-permute-start(f32[4,256]{1,0:T(4,128)S(1)} %get-tuple-element.66), channel_id=1, source_target_pairs={{0,1},{1,0},{2,3},{3,2},{4,5},{5,4},{6,7},{7,6},{8,9},{9,8},{10,11... | collective-permute-start | bytes 12296 | tf_op jit(solution)/shard_map/ppermute | solution.py:464
  22.8 4.3 %collective-permute-start.11 = (f32[4,256]{1,0:T(4,128)S(1)}, f32[4,256]{1,0:T(4,128)S(1)}, u32[]{:S(2)}, u32[]{:S(2)}) collective-permute-start(f32[4,256]{1,0:T(4,128)S(1)} %get-tuple-element.67), channel_id=1, source_target_pairs={{0,4},{1,2},{2,1},{3,7},{4,0},{5,6},{6,5},{7,3},{8,12},{9,10},{10,... | collective-permute-start | bytes 12296 | tf_op jit(solution)/shard_map/ppermute | solution.py:464
  22.8 4.3 %collective-permute-start.12 = (f32[4,256]{1,0:T(4,128)S(1)}, f32[4,256]{1,0:T(4,128)S(1)}, u32[]{:S(2)}, u32[]{:S(2)}) collective-permute-start(f32[4,256]{1,0:T(4,128)S(1)} %get-tuple-element.68), channel_id=1, source_target_pairs={{0,12},{1,13},{2,14},{3,15},{4,8},{5,9},{6,10},{7,11},{8,4},{9,5},... | collective-permute-start | bytes 12296 | tf_op jit(solution)/shard_map/ppermute | solution.py:464
  24.5 3.6 %collective-permute-start.13 = (f32[4,256]{1,0:T(4,128)S(1)}, f32[4,256]{1,0:T(4,128)S(1)}, u32[]{:S(2)}, u32[]{:S(2)}) collective-permute-start(f32[4,256]{1,0:T(4,128)S(1)} %get-tuple-element.69), channel_id=1, source_target_pairs={{0,16},{1,17},{2,18},{3,19},{4,20},{5,21},{6,22},{7,23},{8,24},{9,... | collective-permute-start | bytes 12296 | tf_op jit(solution)/shard_map/ppermute | solution.py:464
  25.2 2.9 %collective-permute-start.14 = (f32[4,256]{1,0:T(4,128)S(1)}, f32[4,256]{1,0:T(4,128)S(1)}, u32[]{:S(2)}, u32[]{:S(2)}) collective-permute-start(f32[4,256]{1,0:T(4,128)S(1)} %get-tuple-element.70), channel_id=1, source_target_pairs={{0,4},{1,5},{2,6},{3,7},{4,0},{5,1},{6,2},{7,3},{8,12},{9,13},{10,... | collective-permute-start | bytes 12296 | tf_op jit(solution)/shard_map/ppermute | solution.py:464
  30.2 6.0 %collective-permute-start.15 = (f32[4,256]{1,0:T(4,128)S(1)}, f32[4,256]{1,0:T(4,128)S(1)}, u32[]{:S(2)}, u32[]{:S(2)}) collective-permute-start(f32[4,256]{1,0:T(4,128)S(1)} %get-tuple-element.76), channel_id=1, source_target_pairs={{0,1},{1,0},{2,3},{3,2},{4,5},{5,4},{6,7},{7,6},{8,9},{9,8},{10,11... | collective-permute-start | bytes 12296 | tf_op jit(solution)/shard_map/ppermute | solution.py:464
  30.7 5.4 %collective-permute-start.16 = (f32[4,256]{1,0:T(4,128)S(1)}, f32[4,256]{1,0:T(4,128)S(1)}, u32[]{:S(2)}, u32[]{:S(2)}) collective-permute-start(f32[4,256]{1,0:T(4,128)S(1)} %get-tuple-element.77), channel_id=1, source_target_pairs={{0,4},{1,2},{2,1},{3,7},{4,0},{5,6},{6,5},{7,3},{8,12},{9,10},{10,... | collective-permute-start | bytes 12296 | tf_op jit(solution)/shard_map/ppermute | solution.py:464
  30.9 5.3 %collective-permute-start.17 = (f32[4,256]{1,0:T(4,128)S(1)}, f32[4,256]{1,0:T(4,128)S(1)}, u32[]{:S(2)}, u32[]{:S(2)}) collective-permute-start(f32[4,256]{1,0:T(4,128)S(1)} %get-tuple-element.78), channel_id=1, source_target_pairs={{0,12},{1,13},{2,14},{3,15},{4,8},{5,9},{6,10},{7,11},{8,4},{9,5},... | collective-permute-start | bytes 12296 | tf_op jit(solution)/shard_map/ppermute | solution.py:464
  32.1 4.1 %collective-permute-start.18 = (f32[4,256]{1,0:T(4,128)S(1)}, f32[4,256]{1,0:T(4,128)S(1)}, u32[]{:S(2)}, u32[]{:S(2)}) collective-permute-start(f32[4,256]{1,0:T(4,128)S(1)} %get-tuple-element.79), channel_id=1, source_target_pairs={{0,16},{1,17},{2,18},{3,19},{4,20},{5,21},{6,22},{7,23},{8,24},{9,... | collective-permute-start | bytes 12296 | tf_op jit(solution)/shard_map/ppermute | solution.py:464
  32.9 3.3 %collective-permute-start.19 = (f32[4,256]{1,0:T(4,128)S(1)}, f32[4,256]{1,0:T(4,128)S(1)}, u32[]{:S(2)}, u32[]{:S(2)}) collective-permute-start(f32[4,256]{1,0:T(4,128)S(1)} %get-tuple-element.80), channel_id=1, source_target_pairs={{0,4},{1,5},{2,6},{3,7},{4,0},{5,1},{6,2},{7,3},{8,12},{9,13},{10,... | collective-permute-start | bytes 12296 | tf_op jit(solution)/shard_map/ppermute | solution.py:464
